TPU v7x, 64 devices: a 2x2x8 block of a 4x4x8 slice. The times are simulated.
64 devices in a mesh: dp: 4 (over x, y), tp: 16 (over z, core).
Axes of the slice: x: 2, y: 2, z: 8, core: 2. Of those that a mesh axis runs over, the one named last changes fastest.
The devices are a block of a 4x4x8 slice.
Arguments:
- hidden: bfloat16 [4, 4096, 4096], P('dp', 'tp'), parts along dimension 0
- attn_gain: float32 [4096], replicated
- w_q: bfloat16 [4096, 4096], P(None, 'tp')
- w_k: bfloat16 [4096, 4096], P(None, 'tp')
- w_v: bfloat16 [4096, 4096], P(None, 'tp')
- q_gain: float32 [4096], P('tp')
- k_gain: float32 [4096], P('tp')
- w_o: bfloat16 [4096, 4096], P('tp')
Outputs:
- output 1: bfloat16 [4, 4096, 4096], P('dp', 'tp'), parts along dimension 0
- output 2: bfloat16 [4, 4096, 32, 128], P('dp', None, 'tp'), parts along dimension 0
- output 3: bfloat16 [4, 4096, 32, 128], P('dp', None, 'tp'), parts along dimension 0
There are 4 independent parts. A program takes and returns all parts, laid end to end along the dimension named above; an argument that names none is the same for every part.
All inputs are finite; a program needn't handle non-finite values.
Results may differ from a plain program's by a relative error of at most 0.0111495.
Values are sent between devices in bfloat16 or wider.
A program may use at most 768 MiB of HBM per device.

v0:
```python
import jax
import jax.numpy as jnp
from jax import lax
from jax.sharding import PartitionSpec as P

HEAD_DIM = 128


def rope_tables(seq_len, head_dim):
    half_dim = head_dim // 2
    inv_freq = 10000.0 ** (-jnp.arange(half_dim, dtype=jnp.float32) * (2.0 / head_dim))
    angles = jnp.arange(seq_len, dtype=jnp.float32)[:, None] * inv_freq[None, :]
    return jnp.cos(angles), jnp.sin(angles)


def apply_rope(heads_in, cos_tab, sin_tab):
    half_dim = heads_in.shape[-1] // 2
    lower_half = heads_in[..., :half_dim]
    upper_half = heads_in[..., half_dim:]
    cos_bcast = cos_tab[None, :, None, :]
    sin_bcast = sin_tab[None, :, None, :]
    return jnp.concatenate([lower_half * cos_bcast - upper_half * sin_bcast, upper_half * cos_bcast + lower_half * sin_bcast], axis=-1)


def causal_attention(q_rot, k_rot, v_heads):
    seq_len = q_rot.shape[1]
    q_tile = min(seq_len, 128)
    score_scale = q_rot.shape[-1] ** -0.5
    tile_outs = []
    for tile_idx in range(seq_len // q_tile):
        q_start = tile_idx * q_tile
        q_stop = q_start + q_tile
        q_part = q_rot[:, q_start:q_stop]
        if tile_outs:
            q_part, prev_out = lax.optimization_barrier((q_part, tile_outs[-1]))
            tile_outs[-1] = prev_out
        scores = jnp.einsum('bqhd,bkhd->bhqk', q_part, k_rot[:, :q_stop], preferred_element_type=jnp.float32) * score_scale
        q_pos = q_start + jnp.arange(q_tile)
        k_pos = jnp.arange(q_stop)
        scores = jnp.where(q_pos[:, None] >= k_pos[None, :], scores, -1e30)
        prob_bf = jax.nn.softmax(scores, axis=-1).astype(jnp.bfloat16)
        tile_out = jnp.einsum('bhqk,bkhd->bqhd', prob_bf, v_heads[:, :q_stop], preferred_element_type=jnp.float32)
        tile_outs.append(tile_out.astype(jnp.bfloat16))
    return jnp.concatenate(tile_outs, axis=1)


def solution(mesh):
    def local_block(x_local, attn_gain, wq_cols, wk_cols, wv_cols, qg_cols, kg_cols, wo_rows):
        n_batch = x_local.shape[0]
        width = x_local.shape[2]
        x_f32 = x_local.astype(jnp.float32)
        inv_rms = lax.rsqrt(jnp.mean(x_f32 * x_f32, axis=-1, keepdims=True) + 1e-5)
        normed = (x_f32 * inv_rms * attn_gain).astype(jnp.bfloat16)
        h_full = lax.all_gather(normed, 'tp', axis=1, tiled=True)
        seq_len = h_full.shape[1]
        local_cols = wq_cols.shape[1]
        local_heads = local_cols // HEAD_DIM
        q_raw = jnp.einsum('btd,dc->btc', h_full, wq_cols, preferred_element_type=jnp.float32).astype(jnp.bfloat16)
        k_raw = jnp.einsum('btd,dc->btc', h_full, wk_cols, preferred_element_type=jnp.float32).astype(jnp.bfloat16)
        v_raw = jnp.einsum('btd,dc->btc', h_full, wv_cols, preferred_element_type=jnp.float32).astype(jnp.bfloat16)
        part_sq = jnp.stack([jnp.einsum('btc,btc->bt', q_raw, q_raw, preferred_element_type=jnp.float32), jnp.einsum('btc,btc->bt', k_raw, k_raw, preferred_element_type=jnp.float32)])
        total_sq = lax.psum(part_sq, 'tp')
        inv_norm = lax.rsqrt(total_sq / width + 1e-5)
        q_normed = q_raw.astype(jnp.float32) * inv_norm[0][..., None] * qg_cols
        k_normed = k_raw.astype(jnp.float32) * inv_norm[1][..., None] * kg_cols
        cos_tab, sin_tab = rope_tables(seq_len, HEAD_DIM)
        head_shape = (n_batch, seq_len, local_heads, HEAD_DIM)
        q_rot = apply_rope(q_normed.reshape(head_shape), cos_tab, sin_tab).astype(jnp.bfloat16)
        k_rot = apply_rope(k_normed.reshape(head_shape), cos_tab, sin_tab).astype(jnp.bfloat16)
        v_heads = v_raw.reshape(head_shape)
        attn_out = causal_attention(q_rot, k_rot, v_heads).reshape(n_batch, seq_len, local_cols)
        y_part = jnp.einsum('btc,cd->btd', attn_out, wo_rows, preferred_element_type=jnp.float32).astype(jnp.bfloat16)
        y_local = lax.psum_scatter(y_part, 'tp', scatter_dimension=1, tiled=True)
        hidden_out = (x_f32 + y_local.astype(jnp.float32)).astype(jnp.bfloat16)
        return (hidden_out, k_rot, v_heads)

    seq_spec = P('dp', 'tp', None)
    head_spec = P('dp', None, 'tp', None)
    col_spec = P(None, 'tp')
    return jax.shard_map(local_block, mesh=mesh, in_specs=(seq_spec, P(None), col_spec, col_spec, col_spec, P('tp'), P('tp'), P('tp', None)), out_specs=(seq_spec, head_spec, head_spec), check_vma=False)
```

profile of v0, /device:TPU:21, one launch (start us, length us, event | category | flops | bytes accessed | tf_op | source)
XLA Modules:
  0.0 893.0 jit_solution(18117974261355965773)
XLA Ops:
  35.9 8.9 fusion.131
  44.8 143.7 %all-gather.2.cloned.1.call-done = bf16[1,4096,4096]{2,1,0:T(8,128)(2,1)} async-done(((bf16[1,256,4096]{2,1,0:T(8,128)(2,1)}), bf16[1,4096,4096]{2,1,0:T(8,128)(2,1)}) %all-gather.2.cloned.1.call-update) | async-done | bytes 33554448 | tf_op jit(solution)/shard_map/all_gather | solution.py:54
  188.6 16.9 %fusion.83 = (f32[4096]{0:T(1024)S(1)}, bf16[4096,256]{0,1:T(8,128)(2,1)}) fusion(bf16[4096,256]{1,0:T(8,128)(2,1)} %param.11, bf16[1,4096,4096]{2,1,0:T(8,128)(2,1)} %all-gather.2.cloned.1.call-done), kind=kOutput, calls=%fused_computation.95 | convolution fusion | flops 8594124800 | bytes 37765120 | tf_op jit(solution)/shard_map/btd,dc->btc/dot_general | solution.py:59
  205.5 16.9 %fusion.82 = (f32[4096]{0:T(1024)S(1)}, bf16[4096,256]{0,1:T(8,128)(2,1)}) fusion(bf16[4096,256]{1,0:T(8,128)(2,1)} %param.10, bf16[1,4096,4096]{2,1,0:T(8,128)(2,1)} %all-gather.2.cloned.1.call-done), kind=kOutput, calls=%fused_computation.94 | convolution fusion | flops 8594124800 | bytes 37765120 | tf_op jit(solution)/shard_map/btd,dc->btc/dot_general | solution.py:58
  222.4 44.1 %psum.7 = f32[2,1,4096]{2,1,0:T(1,128)S(1)} all-reduce(f32[2,1,4096]{2,1,0:T(1,128)S(1)} %pad_maximum_fusion.1), channel_id=1, replica_groups=mesh['dp'=4,'tp'=16] {'tp'}, use_global_device_ids=true, to_apply=%region_1.0 | all-reduce | flops 8192 | bytes 65536 | tf_op jit(solution)/shard_map/psum | solution.py:62
  274.1 3.9 copy.34
  277.9 3.8 copy.32
  281.7 3.7 copy.33
  285.5 3.8 copy.31
  289.2 8.2 subtract_convert_fusion
  301.2 17.0 %fusion.68 = bf16[4096,256]{0,1:T(8,128)(2,1)} fusion(bf16[4096,256]{1,0:T(8,128)(2,1)} %param.12, bf16[1,4096,4096]{2,1,0:T(8,128)(2,1)} %all-gather.2.cloned.1.call-done), kind=kOutput, calls=%fused_computation.80 | convolution fusion | flops 8590983168 | bytes 37748736 | tf_op jit(solution)/shard_map/btd,dc->btc/dot_general | solution.py:60
  408.2 3.7 fusion.226
  418.1 3.7 fusion.227
  425.0 3.6 fusion.117
  428.6 3.9 fusion.228
  435.4 3.9 fusion.126
  439.3 3.9 fusion.229
  446.3 3.9 fusion.79
  450.2 4.2 fusion.221
  457.5 4.1 fusion.80
  461.7 4.2 fusion.242
  469.2 4.2 fusion.89
  473.4 4.4 fusion.241
  481.2 4.4 fusion.90
  485.6 4.4 fusion.240
  493.5 4.5 fusion.91
  498.0 4.6 fusion.239
  502.6 3.8 fusion.588
  506.4 4.6 fusion.92
  511.1 4.7 fusion.238
  515.7 3.7 fusion.591
  519.4 4.7 fusion.93
  524.1 4.9 fusion.237
  529.0 3.8 fusion.594
  532.9 4.9 fusion.102
  537.8 5.0 fusion.236
  542.8 4.3 fusion.597
  547.1 5.0 fusion.46
  552.1 5.1 fusion.235
  557.2 4.0 fusion.600
  561.3 5.1 fusion.47
  566.4 5.1 fusion.234
  571.6 4.2 fusion.603
  575.7 5.2 fusion.48
  580.9 5.5 fusion.216
  586.4 4.3 fusion.606
  590.7 5.4 fusion.49
  596.1 5.4 fusion.215
  601.5 4.4 fusion.609
  605.8 5.4 fusion.50
  611.3 5.6 fusion.214
  616.9 4.7 fusion.612
  621.6 5.6 fusion.51
  627.2 5.6 fusion.233
  632.9 4.6 fusion.615
  637.5 5.7 fusion.52
  643.9 5.9 fusion.232
  671.6 6.5 fusion.618
  678.1 4.3 fusion.231
  682.3 15.6 %convert_bitcast_fusion = bf16[1,4096,4096]{2,1,0:T(8,128)(2,1)} fusion(bf16[4096,256]{0,1:T(8,128)(2,1)} %bitcast.787, bf16[256,4096]{1,0:T(8,128)(2,1)S(1)} %copy-done), kind=kOutput, calls=%fused_computation.38 | convolution fusion | flops 8606711808 | bytes 37748736 | tf_op jit(solution)/shard_map/btc,cd->btd/dot_general | solution.py:72
  698.0 6.2 copy.19
  707.5 18.1 %copy.18 = bf16[1,4096,2,128]{3,2,1,0:T(2,128)(2,1)} copy(bf16[1,4096,2,128]{3,1,2,0:T(8,128)(2,1)S(1)} %pad_maximum_fusion.2) | data formatting | bytes 4194304
  725.7 155.8 %reduce-scatter.2.cloned.1.call-done = bf16[1,256,4096]{2,1,0:T(8,128)(2,1)} async-done(((bf16[1,4096,4096]{2,1,0:T(8,128)(2,1)}), bf16[1,256,4096]{2,1,0:T(8,128)(2,1)}) %reduce-scatter.2.cloned.1.call-update) | async-done | bytes 2097168 | tf_op jit(solution)/shard_map/reduce_scatter | solution.py:73
  881.4 4.3 fusion.88
  (348 shorter events, 183.9 us)
Async XLA Ops:
  7.2 675.2 %copy-start = (bf16[256,4096]{1,0:T(8,128)(2,1)S(1)}, bf16[256,4096]{1,0:T(8,128)(2,1)}, u32[]{:S(2)}) copy-start(bf16[256,4096]{1,0:T(8,128)(2,1)} %param.15) | copy-start | bytes 6291460
  7.2 181.4 %all-gather.2.cloned.1.call-start = ((), (), s32[]{:S(2)}) async-start(), calls=%async_computation.1 | async-start | bytes 35651584 | tf_op jit(solution)/shard_map/all_gather | solution.py:54
  12.4 869.1 %reduce-scatter.2.cloned.1.call-start = ((), (), s32[]{:S(2)}) async-start(), calls=%async_computation.2 | async-start | bytes 35651584 | tf_op jit(solution)/shard_map/reduce_scatter | solution.py:73
  205.5 61.2 %copy-start.91 = (f32[256]{0:T(256)S(1)}, f32[256]{0:T(256)}, u32[]{:S(2)}) copy-start(f32[256]{0:T(256)} %param.13) | copy-start | bytes 3076
  336.6 11.7 %copy-start.36 = (bf16[1,128,2,128]{3,1,2,0:T(8,128)(2,1)}, bf16[1,128,2,128]{3,1,2,0:T(8,128)(2,1)S(1)}, u32[]{:S(2)}) copy-start(bf16[1,128,2,128]{3,1,2,0:T(8,128)(2,1)S(1)} %get-tuple-element.74) | copy-start | bytes 196612
  439.3 4.0 copy-start.53
  450.2 4.2 copy-start.24
  450.2 4.2 copy-start.52
  461.7 4.2 copy-start.23
  461.7 4.2 copy-start.39
  473.4 4.4 copy-start.22
  473.4 4.4 copy-start.51
  485.6 4.5 copy-start.21
  485.6 4.5 copy-start.50
  498.0 4.7 copy-start.20
  498.0 4.7 copy-start.49
  511.1 4.7 copy-start.19
  511.1 4.7 copy-start.48
  524.1 4.9 copy-start.18
  524.1 4.9 copy-start.47
  537.8 5.1 copy-start.17
  537.8 5.1 copy-start.46
  552.1 5.1 copy-start.16
  552.1 5.1 copy-start.45
  566.4 5.2 copy-start.15
  566.4 5.2 copy-start.44
  580.9 5.5 copy-start.14
  580.9 5.5 copy-start.43
  596.1 5.4 copy-start.13
  596.1 5.4 copy-start.42
  611.3 5.6 copy-start.12
  611.3 5.6 copy-start.41
  627.2 5.6 copy-start.11
  627.2 5.6 copy-start.40
  637.5 5.7 copy-start.61
  643.8 6.0 copy-start.62
  643.8 6.8 copy-start.63
  643.8 7.4 copy-start.64
  643.8 8.0 copy-start.65
  643.8 8.7 copy-start.66
  643.8 9.3 %copy-start.67 = (bf16[1,128,2,128]{1,3,2,0:T(8,128)(2,1)S(1)}, bf16[1,128,2,128]{1,3,2,0:T(8,128)(2,1)}, u32[]{:S(2)}) copy-start(bf16[1,128,2,128]{1,3,2,0:T(8,128)(2,1)} %fusion.224) | copy-start | bytes 196612
  643.9 9.9 %copy-start.68 = (bf16[1,128,2,128]{1,3,2,0:T(8,128)(2,1)S(1)}, bf16[1,128,2,128]{1,3,2,0:T(8,128)(2,1)}, u32[]{:S(2)}) copy-start(bf16[1,128,2,128]{1,3,2,0:T(8,128)(2,1)} %fusion.225) | copy-start | bytes 196612
  643.9 10.6 %copy-start.69 = (bf16[1,128,2,128]{1,3,2,0:T(8,128)(2,1)S(1)}, bf16[1,128,2,128]{1,3,2,0:T(8,128)(2,1)}, u32[]{:S(2)}) copy-start(bf16[1,128,2,128]{1,3,2,0:T(8,128)(2,1)} %fusion.243) | copy-start | bytes 196612
  643.9 11.2 %copy-start.70 = (bf16[1,128,2,128]{1,3,2,0:T(8,128)(2,1)S(1)}, bf16[1,128,2,128]{1,3,2,0:T(8,128)(2,1)}, u32[]{:S(2)}) copy-start(bf16[1,128,2,128]{1,3,2,0:T(8,128)(2,1)} %fusion.244) | copy-start | bytes 196612
  643.9 11.8 %copy-start.71 = (bf16[1,128,2,128]{1,3,2,0:T(8,128)(2,1)S(1)}, bf16[1,128,2,128]{1,3,2,0:T(8,128)(2,1)}, u32[]{:S(2)}) copy-start(bf16[1,128,2,128]{1,3,2,0:T(8,128)(2,1)} %fusion.217) | copy-start | bytes 196612
  643.9 12.4 %copy-start.72 = (bf16[1,128,2,128]{1,3,2,0:T(8,128)(2,1)S(1)}, bf16[1,128,2,128]{1,3,2,0:T(8,128)(2,1)}, u32[]{:S(2)}) copy-start(bf16[1,128,2,128]{1,3,2,0:T(8,128)(2,1)} %fusion.218) | copy-start | bytes 196612
  643.9 13.1 %copy-start.73 = (bf16[1,128,2,128]{1,3,2,0:T(8,128)(2,1)S(1)}, bf16[1,128,2,128]{1,3,2,0:T(8,128)(2,1)}, u32[]{:S(2)}) copy-start(bf16[1,128,2,128]{1,3,2,0:T(8,128)(2,1)} %fusion.226) | copy-start | bytes 196612
  643.9 13.7 %copy-start.74 = (bf16[1,128,2,128]{1,3,2,0:T(8,128)(2,1)S(1)}, bf16[1,128,2,128]{1,3,2,0:T(8,128)(2,1)}, u32[]{:S(2)}) copy-start(bf16[1,128,2,128]{1,3,2,0:T(8,128)(2,1)} %fusion.227) | copy-start | bytes 196612
  649.8 12.8 %copy-start.75 = (bf16[1,128,2,128]{1,3,2,0:T(8,128)(2,1)S(1)}, bf16[1,128,2,128]{1,3,2,0:T(8,128)(2,1)}, u32[]{:S(2)}) copy-start(bf16[1,128,2,128]{1,3,2,0:T(8,128)(2,1)} %fusion.242) | copy-start | bytes 196612
  649.8 13.5 %copy-start.76 = (bf16[1,128,2,128]{1,3,2,0:T(8,128)(2,1)S(1)}, bf16[1,128,2,128]{1,3,2,0:T(8,128)(2,1)}, u32[]{:S(2)}) copy-start(bf16[1,128,2,128]{1,3,2,0:T(8,128)(2,1)} %fusion.241) | copy-start | bytes 196612
  649.8 14.1 %copy-start.77 = (bf16[1,128,2,128]{1,3,2,0:T(8,128)(2,1)S(1)}, bf16[1,128,2,128]{1,3,2,0:T(8,128)(2,1)}, u32[]{:S(2)}) copy-start(bf16[1,128,2,128]{1,3,2,0:T(8,128)(2,1)} %fusion.240) | copy-start | bytes 196612
  649.8 14.8 %copy-start.78 = (bf16[1,128,2,128]{1,3,2,0:T(8,128)(2,1)S(1)}, bf16[1,128,2,128]{1,3,2,0:T(8,128)(2,1)}, u32[]{:S(2)}) copy-start(bf16[1,128,2,128]{1,3,2,0:T(8,128)(2,1)} %fusion.239) | copy-start | bytes 196612
  649.8 15.4 %copy-start.79 = (bf16[1,128,2,128]{1,3,2,0:T(8,128)(2,1)S(1)}, bf16[1,128,2,128]{1,3,2,0:T(8,128)(2,1)}, u32[]{:S(2)}) copy-start(bf16[1,128,2,128]{1,3,2,0:T(8,128)(2,1)} %fusion.238) | copy-start | bytes 196612
  649.9 16.0 %copy-start.80 = (bf16[1,128,2,128]{1,3,2,0:T(8,128)(2,1)S(1)}, bf16[1,128,2,128]{1,3,2,0:T(8,128)(2,1)}, u32[]{:S(2)}) copy-start(bf16[1,128,2,128]{1,3,2,0:T(8,128)(2,1)} %fusion.237) | copy-start | bytes 196612
  649.9 16.6 %copy-start.81 = (bf16[1,128,2,128]{1,3,2,0:T(8,128)(2,1)S(1)}, bf16[1,128,2,128]{1,3,2,0:T(8,128)(2,1)}, u32[]{:S(2)}) copy-start(bf16[1,128,2,128]{1,3,2,0:T(8,128)(2,1)} %fusion.236) | copy-start | bytes 196612
  649.9 17.3 %copy-start.82 = (bf16[1,128,2,128]{1,3,2,0:T(8,128)(2,1)S(1)}, bf16[1,128,2,128]{1,3,2,0:T(8,128)(2,1)}, u32[]{:S(2)}) copy-start(bf16[1,128,2,128]{1,3,2,0:T(8,128)(2,1)} %fusion.235) | copy-start | bytes 196612
  649.9 17.9 %copy-start.83 = (bf16[1,128,2,128]{1,3,2,0:T(8,128)(2,1)S(1)}, bf16[1,128,2,128]{1,3,2,0:T(8,128)(2,1)}, u32[]{:S(2)}) copy-start(bf16[1,128,2,128]{1,3,2,0:T(8,128)(2,1)} %fusion.234) | copy-start | bytes 196612
  649.9 18.5 %copy-start.84 = (bf16[1,128,2,128]{1,3,2,0:T(8,128)(2,1)S(1)}, bf16[1,128,2,128]{1,3,2,0:T(8,128)(2,1)}, u32[]{:S(2)}) copy-start(bf16[1,128,2,128]{1,3,2,0:T(8,128)(2,1)} %fusion.216) | copy-start | bytes 196612
  649.9 19.1 %copy-start.85 = (bf16[1,128,2,128]{1,3,2,0:T(8,128)(2,1)S(1)}, bf16[1,128,2,128]{1,3,2,0:T(8,128)(2,1)}, u32[]{:S(2)}) copy-start(bf16[1,128,2,128]{1,3,2,0:T(8,128)(2,1)} %fusion.215) | copy-start | bytes 196612
  649.9 19.8 %copy-start.86 = (bf16[1,128,2,128]{1,3,2,0:T(8,128)(2,1)S(1)}, bf16[1,128,2,128]{1,3,2,0:T(8,128)(2,1)}, u32[]{:S(2)}) copy-start(bf16[1,128,2,128]{1,3,2,0:T(8,128)(2,1)} %fusion.214) | copy-start | bytes 196612
  649.9 20.4 %copy-start.87 = (bf16[1,128,2,128]{1,3,2,0:T(8,128)(2,1)S(1)}, bf16[1,128,2,128]{1,3,2,0:T(8,128)(2,1)}, u32[]{:S(2)}) copy-start(bf16[1,128,2,128]{1,3,2,0:T(8,128)(2,1)} %fusion.233) | copy-start | bytes 196612
  649.9 21.0 %copy-start.88 = (bf16[1,128,2,128]{1,3,2,0:T(8,128)(2,1)S(1)}, bf16[1,128,2,128]{1,3,2,0:T(8,128)(2,1)}, u32[]{:S(2)}) copy-start(bf16[1,128,2,128]{1,3,2,0:T(8,128)(2,1)} %fusion.232) | copy-start | bytes 196612
  649.9 21.7 %copy-start.38 = (pred[128,4096]{1,0:T(8,128)(4,1)S(1)}, pred[128,4096]{1,0:T(8,128)(4,1)}, u32[]{:S(2)}) copy-start(pred[128,4096]{1,0:T(8,128)(4,1)} %iota_compare_fusion) | copy-start | bytes 1572868
  650.0 21.6 %copy-start.60 = (bf16[1,128,2,128]{3,1,2,0:T(8,128)(2,1)S(1)}, bf16[1,128,2,128]{3,1,2,0:T(8,128)(2,1)}, u32[]{:S(2)}) copy-start(bf16[1,128,2,128]{3,1,2,0:T(8,128)(2,1)} %pad_maximum_fusion) | copy-start | bytes 196612
  (31 other events, 87.5 us)
Sparse Core Ops, SparseCore 0:
  12.5 176.0 all-gather.1
  698.1 183.2 reduce-scatter.1
where the time goes:
time: 901 us; the launch traced here: 893 us
  matrix products  404 us (45%)
  waiting for transfers between devices  300 us (33%)
  local copies, waits for them, and re-layouts  70 us (8%)
  other arithmetic  60.2 us (7%)
  blocking collectives  44.1 us (5%)
  between operations  15.3 us (2%)
    reduce_scatter x1, waiting for transfers between devices, local_block(): y_local = lax.psum_scatter(y_part, 'tp', scatter_dimension=1, tiled=True)  156 us
    all_gather x1, waiting for transfers between devices, local_block(): h_full = lax.all_gather(normed, 'tp', axis=1, tiled=True)  144 us
    dot_general x32, matrix products, causal_attention(): jnp.einsum('bhqk,bkhd->bqhd', prob_bf, v_heads[:, :q_stop], preferred_ele...  126 us
    dot_general x31, matrix products, causal_attention(): jnp.einsum('bqhd,bkhd->bhqk', q_part, k_rot[:, :q_stop], preferred_elemen...  113 us
    sub x31, matrix products, causal_attention(): prob_bf = jax.nn.softmax(scores, axis=-1).astype(jnp.bfloat16)  97.8 us
    unnamed x223, local copies, waits for them, and re-layouts  65.4 us
    psum x1, blocking collectives, local_block(): total_sq = lax.psum(part_sq, 'tp')  44.1 us
    ge x32, other arithmetic, causal_attention(): scores = jnp.where(q_pos[:, None] >= k_pos[None, :], scores, -1e+30)  23.1 us
  transfers between devices with their start and end apart: 2, of which 2 were waited for; matrix products, arithmetic and copies ran while one was open for 7% of the time, Pallas kernels for 0%

commit v1 on v0

v1 whole, which is shorter than its diff:
```python
import functools
import math

import jax
import jax.numpy as jnp
import numpy as np
from jax import lax
from jax.experimental import pallas as pl
from jax.experimental.pallas import tpu as pltpu
from jax.sharding import PartitionSpec as P

HEAD_DIM = 128
EPS = 1e-5
PIECE = 64
SUM_PIECES = 4
F32 = jnp.float32
BF16 = jnp.bfloat16


def rope_constants(seq_len):
    half = HEAD_DIM // 2
    inv_freq = 10000.0 ** (-np.arange(half) * (2.0 / HEAD_DIM))
    inv_freq = np.concatenate([inv_freq, inv_freq])
    sign = np.concatenate([-np.ones(half), np.ones(half)])
    base = (np.arange(seq_len // PIECE) * PIECE)[:, None] * inv_freq
    off = np.arange(PIECE)[:, None] * inv_freq
    return [jnp.asarray(t, F32) for t in (np.cos(base), sign * np.sin(base), np.cos(off), sign * np.sin(off))]


def block_kernel(
    n, x_hbm, gain, wq_hbm, wk_hbm, wv_hbm, wo_hbm, q_gain, k_gain, cos_b, sin_b, cos_o, sin_o,
    out_hbm, k_hbm, v_hbm,
    hbuf, wqkv, wo, q_s, k_s, v_s, x_s, ybuf, o_s, sq_out, sq_in, inv,
    ld_sem, ag_send, ag_recv, dd_send, dd_recv, sq_send, sq_recv, iv_send, iv_recv,
    rs_send, rs_recv, sb_send, sb_recv, st_sem,
):
    nz = n // 2
    me = lax.axis_index("tp")
    z, c = me // 2, lax.rem(me, 2)
    sib = z * 2 + 1 - c
    n_rows, width = x_s.shape
    half = n_rows // 2
    pieces = half // PIECE
    units = nz * pieces
    cols = q_s.shape[1]
    heads = cols // HEAD_DIM
    sub = half // SUM_PIECES
    k_tile = 2 * n_rows

    def chip(offset):
        return lax.rem(z + offset + 2 * nz, nz)

    def toward(d, hops=1):
        return chip(hops) if d == 0 else chip(-hops)

    def rows(start, size):
        return pl.ds(pl.multiple_of(start, size), size)

    def remote(src, dst, send, recv, dev):
        return pltpu.make_async_remote_copy(
            src_ref=src, dst_ref=dst, send_sem=send, recv_sem=recv,
            device_id={"tp": dev}, device_id_type=pl.DeviceIdType.MESH)

    loads = [pltpu.make_async_copy(x_hbm, x_s, ld_sem.at[0])]
    for i, w in enumerate((wq_hbm, wk_hbm, wv_hbm)):
        loads.append(pltpu.make_async_copy(w, wqkv.at[i], ld_sem.at[1 + i]))
    loads.append(pltpu.make_async_copy(wo_hbm, wo, ld_sem.at[4]))
    for load in loads:
        load.start()

    barrier = pltpu.get_barrier_semaphore()

    def greet(i, _):
        pl.semaphore_signal(barrier, inc=1, device_id={"tp": lax.rem(me + i, n)}, device_id_type=pl.DeviceIdType.MESH)
        return 0

    lax.fori_loop(1, n, greet, 0)

    def quarter(u, d):
        return hbuf.at[u, rows((2 * d + c) * PIECE, PIECE)]

    def ring_copy(u, d):
        return remote(quarter(u, d), quarter(u + pieces, d), ag_send.at[u, d], ag_recv.at[u, d], toward(d) * 2 + c)

    def pair_copy(u, d):
        return remote(quarter(u, d), quarter(u, d), dd_send.at[u, d], dd_recv.at[u, d], sib)

    loads[0].wait()
    for p in range(pieces):
        for d in range(2):
            x = x_s[pl.ds(d * half + p * PIECE, PIECE), :].astype(F32)
            inv_rms = lax.rsqrt(jnp.mean(x * x, axis=-1, keepdims=True) + EPS)
            hbuf[p, rows((2 * d + c) * PIECE, PIECE), :] = (x * inv_rms * gain[...]).astype(BF16)
        if p == 0:
            pl.semaphore_wait(barrier, n - 1)
        for d in range(2):
            ring_copy(p, d).start()
            pair_copy(p, d).start()

    def sq_copy(u, d, p, dev):
        return remote(sq_out.at[u, d], sq_in.at[me, p], sq_send.at[u, d], sq_recv.at[me, p], dev)

    def project(v):
        s, p = v // pieces, lax.rem(v, pieces)
        for d in range(2):
            pair_copy(v, d).wait_recv()

        @pl.when(v == 0)
        def _():
            for load in loads[1:]:
                load.wait()

        h = hbuf[v]
        sums = []
        for i, dst in enumerate((q_s, k_s, v_s)):
            out = jnp.dot(h, wqkv[i], preferred_element_type=F32).astype(BF16)
            for d in range(2):
                src = chip(-s) if d == 0 else chip(s)
                for cc in range(2):
                    at = (2 * src + cc) * n_rows + d * half + p * PIECE
                    lo = (2 * d + cc) * PIECE
                    dst[rows(at, PIECE), :] = out[lo:lo + PIECE]
            if i < 2:
                wide = out.astype(F32)
                sq = wide * wide
                lanes = sq[:, :HEAD_DIM]
                for j in range(1, heads):
                    lanes = lanes + sq[:, j * HEAD_DIM:(j + 1) * HEAD_DIM]
                sums.append(lanes)
        for d in range(2):
            for i in range(2):
                part = sums[i][d * 2 * PIECE:(d + 1) * 2 * PIECE]
                sq_out[v, d, pl.ds(i, 1), :] = jnp.sum(part.T, axis=0, keepdims=True)
            owner = chip(-s - 1) if d == 0 else chip(s + 1)

            @pl.when(s < nz - 1)
            def _(d=d, owner=owner):
                sq_copy(v, d, p, owner * 2 + d).start()

            @pl.when((s == nz - 1) & (c != d))
            def _(d=d):
                sq_copy(v, d, p, sib).start()

            @pl.when((s == nz - 1) & (c == d))
            def _(d=d):
                sq_in[me, p] = sq_out[v, d]

    def gather_step(u, _):
        @pl.when((u >= pieces) & (u < units))
        def _():
            for d in range(2):
                ring_copy(u - pieces, d).wait_recv()

                @pl.when(u < units - pieces)
                def _(d=d):
                    ring_copy(u, d).start()

                pair_copy(u, d).start()

        project(u - 1)
        return 0

    lax.fori_loop(1, units + 1, gather_step, 0)

    v_out = pltpu.make_async_copy(v_s, v_hbm, st_sem.at[0])
    v_out.start()

    def drain_gather(u, _):
        for d in range(2):
            pair_copy(u, d).wait_send()

            @pl.when(u < units - pieces)
            def _(d=d):
                ring_copy(u, d).wait_send()
                sq_copy(u, d, 0, sib).wait_send()

            @pl.when((u >= units - pieces) & (c != d))
            def _(d=d):
                sq_copy(u, d, 0, sib).wait_send()

        return 0

    lax.fori_loop(0, units, drain_gather, 0)

    def sq_arrived(i, _):
        peer = lax.rem(me + i, n)
        for p in range(pieces):
            remote(sq_out.at[0, 0], sq_in.at[peer, p], sq_send.at[0, 0], sq_recv.at[peer, p], sib).wait_recv()
        return 0

    lax.fori_loop(1, n, sq_arrived, 0)
    total = sq_in[0]
    for i in range(1, n):
        total = total + sq_in[i]
    inv[me] = lax.rsqrt(total / (cols * n) + EPS)

    def inv_copy(i):
        dev = lax.rem(me + i, n)
        return remote(inv.at[me], inv.at[me], iv_send.at[i], iv_recv.at[me], dev)

    def inv_start(i, _):
        inv_copy(i).start()
        return 0

    def inv_wait(i, _):
        peer = lax.rem(me + i, n)
        remote(inv.at[peer], inv.at[peer], iv_send.at[i], iv_recv.at[peer], sib).wait_recv()
        return 0

    def inv_sent(i, _):
        inv_copy(i).wait_send()
        return 0

    lax.fori_loop(1, n, inv_start, 0)
    lax.fori_loop(1, n, inv_wait, 0)
    lax.fori_loop(1, n, inv_sent, 0)

    def normed_rope(raw, which, src, d, p):
        own = lax.rem(src + (nz - 1 if d == 0 else 1), nz) * 2 + d
        scale = inv[own, p][which:which + 1]
        scale = jnp.broadcast_to(scale, (HEAD_DIM, HEAD_DIM)).T
        gains = (q_gain, k_gain)[which][...]
        done = []
        for cc in range(2):
            b = (2 * src + cc) * (n_rows // PIECE) + d * pieces + p
            cb, sb = cos_b[pl.ds(b, 1), :], sin_b[pl.ds(b, 1), :]
            cos = cb * cos_o[...] - sb * sin_o[...]
            sin = sb * cos_o[...] + cb * sin_o[...]
            out = []
            for j in range(heads):
                lanes = slice(j * HEAD_DIM, (j + 1) * HEAD_DIM)
                t = raw[cc][:, lanes].astype(F32) * scale[cc * PIECE:(cc + 1) * PIECE] * gains[:, lanes]
                out.append((t * cos + pltpu.roll(t, HEAD_DIM // 2, 1) * sin).astype(BF16))
            done.append(out)
        return done

    def finish_keys(src, _):
        for d in range(2):
            for p in range(pieces):
                at = [rows((2 * src + cc) * n_rows + d * half + p * PIECE, PIECE) for cc in range(2)]
                done = normed_rope([k_s[r, :] for r in at], 1, src, d, p)
                for cc in range(2):
                    for j in range(heads):
                        k_s[at[cc], j * HEAD_DIM:(j + 1) * HEAD_DIM] = done[cc][j]
        return 0

    lax.fori_loop(0, nz, finish_keys, 0)
    k_out = pltpu.make_async_copy(k_s, k_hbm, st_sem.at[1])
    k_out.start()

    scale = HEAD_DIM ** -0.5 * math.log2(math.e)

    def attend(t, d):
        blk = lax.rem(z + 2 * nz - 1 - t, nz) if d == 0 else lax.rem(z + 1 + t, nz)
        parts = [[None] * pieces for _ in range(2)]
        for p in range(pieces):
            at = [rows((2 * blk + cc) * n_rows + d * half + p * PIECE, PIECE) for cc in range(2)]
            done = normed_rope([q_s[r, :] for r in at], 0, blk, d, p)
            for cc in range(2):
                parts[cc][p] = done[cc]
        q = [jnp.concatenate([parts[cc][p][j] for cc in range(2) for p in range(pieces)], axis=0) for j in range(heads)]

        def tile(j, at, m, l, acc, mask):
            lanes = slice(j * HEAD_DIM, (j + 1) * HEAD_DIM)
            sc = lax.dot_general(q[j], k_s[at, lanes], (((1,), (1,)), ((), ())), preferred_element_type=F32) * scale
            if mask is not None:
                sc = jnp.where(mask, sc, -1e30)
            m_new = jnp.maximum(m, jnp.max(sc, axis=1, keepdims=True))
            prob = jnp.exp2(sc - m_new)
            fade = jnp.exp2(m - m_new)
            l = l * fade + jnp.sum(prob, axis=1, keepdims=True)
            acc = acc * fade + jnp.dot(prob.astype(BF16), v_s[at, lanes], preferred_element_type=F32)
            return m_new, l, acc

        def step(i, carry):
            at = rows(i * k_tile, k_tile)
            return tuple(tile(j, at, *carry[j], None) for j in range(heads))

        zero = (jnp.full((n_rows, 1), -1e30, F32), jnp.zeros((n_rows, 1), F32), jnp.zeros((n_rows, HEAD_DIM), F32))
        carry = lax.fori_loop(0, blk, step, (zero,) * heads)
        r = lax.broadcasted_iota(jnp.int32, (n_rows, k_tile), 0)
        col = lax.broadcasted_iota(jnp.int32, (n_rows, k_tile), 1)
        mask = jnp.where(r < half, r, r + (n_rows - half)) + d * half >= col
        at = rows(blk * k_tile, k_tile)
        for j in range(heads):
            _, l, acc = tile(j, at, *carry[j], mask)
            o_s[d, :, j * HEAD_DIM:(j + 1) * HEAD_DIM] = (acc / l).astype(BF16)

    def share_copy(t, d):
        return remote(
            ybuf.at[lax.rem(t, 2), 1 - c, d], hbuf.at[nz * pieces // 2 + t, pl.ds(d * half, half)],
            sb_send.at[t, d], sb_recv.at[t, d], sib)

    y_tile = min(width, 1024)

    def emit(t, d):
        slot = lax.rem(t, 2)

        @pl.when(t >= 2)
        def _():
            share_copy(t - 2, d).wait_send()

        def column(i, _):
            at = rows(i * y_tile, y_tile)
            y = jnp.dot(o_s[d], wo[:, at], preferred_element_type=F32).astype(BF16)
            ybuf[slot, 0, d, :, at] = y[:half]
            ybuf[slot, 1, d, :, at] = y[half:]
            return 0

        lax.fori_loop(0, width // y_tile, column, 0)
        share_copy(t, d).start()

    def sum_copy(s, d, k):
        at = rows(d * half + k * sub, sub)
        return remote(hbuf.at[s, at], hbuf.at[s + 1, at], rs_send.at[s, d * SUM_PIECES + k],
                      rs_recv.at[s, d * SUM_PIECES + k], toward(d) * 2 + c)

    def out_copy(d, k):
        at = rows(d * half + k * sub, sub)
        return pltpu.make_async_copy(hbuf.at[nz - 1, at], out_hbm.at[at], st_sem.at[2 + d * SUM_PIECES + k])

    def add_up(s, k):
        for d in range(2):
            if k == 0:
                share_copy(s, d).wait_recv()

            @pl.when(s >= 1)
            def _(d=d):
                sum_copy(s - 1, d, k).wait_recv()

            at = rows(d * half + k * sub, sub)

            def column(i, _, d=d, at=at):
                lanes = rows(i * y_tile, y_tile)
                y = ybuf[lax.rem(s, 2), c, d, pl.ds(k * sub, sub), lanes].astype(F32)
                y = y + hbuf[nz * pieces // 2 + s, at, lanes].astype(F32)
                run = hbuf[s, at, lanes].astype(F32)
                y = (y + jnp.where(s >= 1, run, 0.0)).astype(BF16)
                hbuf[s, at, lanes] = y

                @pl.when(s == nz - 1)
                def _():
                    hbuf[s, at, lanes] = (x_s[at, lanes].astype(F32) + y.astype(F32)).astype(BF16)

                return 0

            lax.fori_loop(0, width // y_tile, column, 0)

            @pl.when(s < nz - 1)
            def _(d=d):
                sum_copy(s, d, k).start()

            @pl.when(s == nz - 1)
            def _(d=d):
                out_copy(d, k).start()

    def scatter_step(t, _):
        for k in range(SUM_PIECES):
            @pl.when(t >= 1)
            def _(k=k):
                add_up(t - 1, k)

            @pl.when(t < nz)
            def _(k=k):
                if k % 2 == 0:
                    attend(t, k // 2)
                else:
                    emit(t, k // 2)

        return 0

    lax.fori_loop(0, nz + 1, scatter_step, 0)

    def drain_scatter(s, _):
        for d in range(2):
            for k in range(SUM_PIECES):
                sum_copy(s, d, k).wait_send()
        return 0

    lax.fori_loop(0, nz - 1, drain_scatter, 0)
    for d in range(2):
        for t in (nz - 2, nz - 1):
            share_copy(t, d).wait_send()
        for k in range(SUM_PIECES):
            out_copy(d, k).wait()
    v_out.wait()
    k_out.wait()


def solution(mesh):
    n = mesh.shape["tp"]

    def local_block(x_local, attn_gain, wq, wk, wv, q_gain, k_gain, wo):
        _, n_rows, width = x_local.shape
        cols = wq.shape[1]
        seq_len = n * n_rows
        nz, pieces = n // 2, n_rows // 2 // PIECE
        units = nz * pieces
        tables = rope_constants(seq_len)
        any_spec = pl.BlockSpec(memory_space=pl.ANY)
        vmem_spec = pl.BlockSpec(memory_space=pltpu.VMEM)
        dma = pltpu.SemaphoreType.DMA
        out, k_rot, v_rows = pl.pallas_call(
            functools.partial(block_kernel, n),
            out_shape=(
                jax.ShapeDtypeStruct((n_rows, width), BF16),
                jax.ShapeDtypeStruct((seq_len, cols), BF16),
                jax.ShapeDtypeStruct((seq_len, cols), BF16),
            ),
            in_specs=[any_spec, vmem_spec] + [any_spec] * 4 + [vmem_spec] * 6,
            out_specs=(any_spec,) * 3,
            scratch_shapes=[
                pltpu.VMEM((units, 4 * PIECE, width), BF16),
                pltpu.VMEM((3, width, cols), BF16),
                pltpu.VMEM((cols, width), BF16),
                pltpu.VMEM((seq_len, cols), BF16),
                pltpu.VMEM((seq_len, cols), BF16),
                pltpu.VMEM((seq_len, cols), BF16),
                pltpu.VMEM((n_rows, width), BF16),
                pltpu.VMEM((2, 2, 2, n_rows // 2, width), BF16),
                pltpu.VMEM((2, n_rows, cols), BF16),
                pltpu.VMEM((units, 2, 2, 2 * PIECE), F32),
                pltpu.VMEM((n, pieces, 2, 2 * PIECE), F32),
                pltpu.VMEM((n, pieces, 2, 2 * PIECE), F32),
                dma((5,)),
                dma((units, 2)), dma((units, 2)), dma((units, 2)), dma((units, 2)),
                dma((units, 2)), dma((n, pieces)), dma((n,)), dma((n,)),
                dma((nz - 1, 2 * SUM_PIECES)), dma((nz - 1, 2 * SUM_PIECES)),
                dma((nz, 2)), dma((nz, 2)), dma((2 + 2 * SUM_PIECES,)),
            ],
            compiler_params=pltpu.CompilerParams(
                collective_id=0, has_side_effects=True, vmem_limit_bytes=67043328),
            name="attention_block",
        )(x_local[0], attn_gain[None], wq, wk, wv, wo, q_gain[None], k_gain[None], *tables)
        head_shape = (1, seq_len, cols // HEAD_DIM, HEAD_DIM)
        return out[None], k_rot.reshape(head_shape), v_rows.reshape(head_shape)

    seq_spec = P("dp", "tp", None)
    head_spec = P("dp", None, "tp", None)
    col_spec = P(None, "tp")
    return jax.shard_map(
        local_block, mesh=mesh,
        in_specs=(seq_spec, P(None), col_spec, col_spec, col_spec, P("tp"), P("tp"), P("tp", None)),
        out_specs=(seq_spec, head_spec, head_spec), check_vma=False)
```

time: 901 us -> 374 us (0.42)
  matrix products: 404 us -> 0 us
  Pallas kernels: 0 us -> 363 us
  waiting for transfers between devices: 300 us -> 0 us
  local copies, waits for them, and re-layouts: 70 us -> 9.38 us
  other arithmetic: 60.2 us -> 0 us
  blocking collectives: 44.1 us -> 0 us
  between operations: 15.3 us -> 0.64 us
    pallas_call x0 -> x1, Pallas kernels: none -> 363 us  [local_block(): pl.pallas_call(functools.partial(block_kernel, n), out_shape=(jax.ShapeDt...]
    dot_general x67 -> x0, matrix products: 306 us -> none  [the longest x32 126 us: causal_attention(): jnp.einsum('bhqk,bkhd->bqhd', prob_bf, v_heads[:, :q_stop], preferred_ele...]
    reduce_scatter x1 -> x0, waiting for transfers between devices: 156 us -> none  [local_block(): y_local = lax.psum_scatter(y_part, 'tp', scatter_dimension=1, tiled=True)]
    all_gather x1 -> x0, waiting for transfers between devices: 144 us -> none  [local_block(): h_full = lax.all_gather(normed, 'tp', axis=1, tiled=True)]
    sub x31 -> x0, matrix products: 97.8 us -> none  [causal_attention(): prob_bf = jax.nn.softmax(scores, axis=-1).astype(jnp.bfloat16)]
    unnamed x223 -> x3, local copies, waits for them, and re-layouts: 65.4 us -> 1.32 us
    psum x1 -> x0, blocking collectives: 44.1 us -> none  [local_block(): total_sq = lax.psum(part_sq, 'tp')]
    ge x32 -> x0, other arithmetic: 23.1 us -> none  [causal_attention(): scores = jnp.where(q_pos[:, None] >= k_pos[None, :], scores, -1e+30)]
  transfers between devices with their start and end apart: 2 -> 0, of which waited for: 2 -> 0; matrix products, arithmetic and copies ran while one was open for 7% -> 0% of each run, Pallas kernels for 0% -> 0%
where the time goes in v1:
time: 374 us; the launch traced here: 373 us
  Pallas kernels  363 us (97%)
  local copies, waits for them, and re-layouts  9.38 us (3%)
    pallas_call x1, Pallas kernels, local_block(): pl.pallas_call(functools.partial(block_kernel, n), out_shape=(jax.ShapeDt...  363 us
    reshape x2, local copies, waits for them, and re-layouts, local_block(): return (out[None], k_rot.reshape(head_shape), v_rows.reshape(head_shape))  8.06 us

profile of v1, /device:TPU:21, one launch (start us, length us, event | category | flops | bytes accessed | tf_op | source)
XLA Modules:
  0.0 372.9 jit_solution(4584071894616169671)
XLA Ops:
  0.6 362.9 %attention_block.1 = (bf16[256,4096]{1,0:T(8,128)(2,1)}, bf16[4096,256]{1,0:T(8,128)(2,1)}, bf16[4096,256]{1,0:T(8,128)(2,1)}) custom-call(bf16[256,4096]{1,0:T(8,128)(2,1)} %bitcast.6, f32[1,4096]{1,0:T(1,128)} %bitcast.7, bf16[4096,256]{1,0:T(8,128)(2,1)} %wq_hbm.1, bf16[4096,256]{1,0:T(8,128)(2,1)} %wk_hbm.1, bf16[4096,256]{1,0:T(8,128)(2,1)} %wv_hbm.1, ...), custom_call_target="tpu_custom_call" | custom-call | tf_op jit(solution)/shard_map/attention_block/pallas_call | solution.py:403
  363.5 4.0 %reshape.12 = bf16[1,4096,2,128]{3,2,1,0:T(2,128)(2,1)} reshape(bf16[4096,256]{1,0:T(8,128)(2,1)} %get-tuple-element.7) | data formatting | bytes 4194304 | tf_op jit(solution)/shard_map/reshape | solution.py:436
  367.5 0.0 copy-start
  367.5 4.1 %reshape.13 = bf16[1,4096,2,128]{3,2,1,0:T(2,128)(2,1)} reshape(bf16[4096,256]{1,0:T(8,128)(2,1)} %get-tuple-element.8) | data formatting | bytes 4194304 | tf_op jit(solution)/shard_map/reshape | solution.py:436
  371.6 0.0 copy-done
  371.6 1.3 copy.16
Async XLA Ops:
  367.5 4.1 %copy-start = (bf16[256,4096]{1,0:T(8,128)(2,1)S(1)}, bf16[256,4096]{1,0:T(8,128)(2,1)}, u32[]{:S(2)}) copy-start(bf16[256,4096]{1,0:T(8,128)(2,1)} %get-tuple-element.6) | copy-start | bytes 6291460

commit v2 on v1

v2 whole, which is shorter than its diff:
```python
import functools
import math

import jax
import jax.numpy as jnp
import numpy as np
from jax import lax
from jax.experimental import pallas as pl
from jax.experimental.pallas import tpu as pltpu
from jax.sharding import PartitionSpec as P

HEAD_DIM = 128
EPS = 1e-5
PIECE = 64
SUM_PIECES = 4
F32 = jnp.float32
BF16 = jnp.bfloat16


def rope_constants(seq_len):
    half = HEAD_DIM // 2
    inv_freq = 10000.0 ** (-np.arange(half) * (2.0 / HEAD_DIM))
    inv_freq = np.concatenate([inv_freq, inv_freq])
    sign = np.concatenate([-np.ones(half), np.ones(half)])
    base = (np.arange(seq_len // PIECE) * PIECE)[:, None] * inv_freq
    off = np.arange(PIECE)[:, None] * inv_freq
    return [jnp.asarray(t, F32) for t in (np.cos(base), sign * np.sin(base), np.cos(off), sign * np.sin(off))]


def block_kernel(
    n, x_hbm, gain, wq_hbm, wk_hbm, wv_hbm, wo_hbm, q_gain, k_gain, cos_b, sin_b, cos_o, sin_o,
    out_hbm, k_hbm, v_hbm,
    hbuf, wqkv, wo, q_s, k_f, k_s, v_s, v_t, ybuf, o_s, kv_st, sq_out, sq_in, inv,
    ld_sem, ag_send, ag_recv, dd_send, dd_recv, sq_send, sq_recv, iv_send, iv_recv,
    rs_send, rs_recv, sb_send, sb_recv, st_sem, out_sem,
):
    nz = n // 2
    me = lax.axis_index("tp")
    z, c = me // 2, lax.rem(me, 2)
    sib = z * 2 + 1 - c
    n_rows, width = x_hbm.shape
    half = n_rows // 2
    pieces = half // PIECE
    units = nz * pieces
    cols = q_s.shape[1]
    heads = cols // HEAD_DIM
    sub = half // SUM_PIECES
    k_tile = 2 * n_rows
    shares = units // 2
    cast_rows = q_s.shape[0] // (nz * SUM_PIECES)

    def chip(offset):
        return lax.rem(z + offset + 2 * nz, nz)

    def toward(d, hops=1):
        return chip(hops) if d == 0 else chip(-hops)

    def rows(start, size):
        return pl.ds(pl.multiple_of(start, size), size)

    def remote(src, dst, send, recv, dev):
        return pltpu.make_async_remote_copy(
            src_ref=src, dst_ref=dst, send_sem=send, recv_sem=recv,
            device_id={"tp": dev}, device_id_type=pl.DeviceIdType.MESH)

    def x_load(d, p):
        at = pl.ds(d * half + p * PIECE, PIECE)
        return pltpu.make_async_copy(x_hbm.at[at], ybuf.at[0, d, pl.ds(p * PIECE, PIECE)], ld_sem.at[4 + d * pieces + p])

    for p in range(pieces):
        for d in range(2):
            x_load(d, p).start()
    loads = [pltpu.make_async_copy(w, wqkv.at[i], ld_sem.at[i]) for i, w in enumerate((wq_hbm, wk_hbm, wv_hbm))]
    loads.append(pltpu.make_async_copy(wo_hbm, wo, ld_sem.at[3]))

    barrier = pltpu.get_barrier_semaphore()

    def greet(i, _):
        pl.semaphore_signal(barrier, inc=1, device_id={"tp": lax.rem(me + i, n)}, device_id_type=pl.DeviceIdType.MESH)
        return 0

    lax.fori_loop(1, n, greet, 0)

    def quarter(u, d):
        return hbuf.at[u, rows((2 * d + c) * PIECE, PIECE)]

    def ring_copy(u, d):
        return remote(quarter(u, d), quarter(u + pieces, d), ag_send.at[u, d], ag_recv.at[u, d], toward(d) * 2 + c)

    def pair_copy(u, d):
        return remote(quarter(u, d), quarter(u, d), dd_send.at[u, d], dd_recv.at[u, d], sib)

    for p in range(pieces):
        for d in range(2):
            x_load(d, p).wait()
            x = ybuf[0, d, pl.ds(p * PIECE, PIECE), :].astype(F32)
            inv_rms = lax.rsqrt(jnp.mean(x * x, axis=-1, keepdims=True) + EPS)
            hbuf[p, rows((2 * d + c) * PIECE, PIECE), :] = (x * inv_rms * gain[...]).astype(BF16)
        if p == 0:
            for load in loads:
                load.start()
            pl.semaphore_wait(barrier, n - 1)
        for d in range(2):
            ring_copy(p, d).start()
            pair_copy(p, d).start()

    def sq_copy(u, d, p, dev):
        return remote(sq_out.at[u, d], sq_in.at[me, p], sq_send.at[u, d], sq_recv.at[me, p], dev)

    def rotate(t, src, d, cc, p):
        b = (2 * src + cc) * (n_rows // PIECE) + d * pieces + p
        cb, sb = cos_b[pl.ds(b, 1), :], sin_b[pl.ds(b, 1), :]
        cos = cb * cos_o[...] - sb * sin_o[...]
        sin = sb * cos_o[...] + cb * sin_o[...]
        heads_in = [t[:, j * HEAD_DIM:(j + 1) * HEAD_DIM] for j in range(heads)]
        return [x * cos + pltpu.roll(x, HEAD_DIM // 2, 1) * sin for x in heads_in]

    def project(v):
        s, p = v // pieces, lax.rem(v, pieces)
        for d in range(2):
            pair_copy(v, d).wait_recv()

        @pl.when(v == 0)
        def _():
            for load in loads:
                load.wait()

        h = hbuf[v]
        parts = [(d, cc, chip(-s) if d == 0 else chip(s), (2 * d + cc) * PIECE) for d in range(2) for cc in range(2)]

        def at(d, cc, src):
            return rows((2 * src + cc) * n_rows + d * half + p * PIECE, PIECE)

        outs, sums = [], []
        for i in range(2):
            out = jnp.dot(h, wqkv[i], preferred_element_type=F32).astype(BF16)
            wide = out.astype(F32)
            sq = wide * wide
            lanes = sq[:, :HEAD_DIM]
            for j in range(1, heads):
                lanes = lanes + sq[:, j * HEAD_DIM:(j + 1) * HEAD_DIM]
            outs.append(out)
            sums.append(lanes)
        for d, cc, src, lo in parts:
            q_s[at(d, cc, src), :] = outs[0][lo:lo + PIECE]
            k_f[at(d, cc, src), :] = outs[1][lo:lo + PIECE].astype(F32)
        for d in range(2):
            for i in range(2):
                part = sums[i][d * 2 * PIECE:(d + 1) * 2 * PIECE]
                sq_out[v, d, pl.ds(i, 1), :] = jnp.sum(part.T, axis=0, keepdims=True)
            owner = chip(-s - 1) if d == 0 else chip(s + 1)

            @pl.when(s < nz - 1)
            def _(d=d, owner=owner):
                sq_copy(v, d, p, owner * 2 + d).start()

            @pl.when((s == nz - 1) & (c != d))
            def _(d=d):
                sq_copy(v, d, p, sib).start()

            @pl.when((s == nz - 1) & (c == d))
            def _(d=d):
                sq_in[me, p] = sq_out[v, d]

    def project_rest(v):
        s, p = v // pieces, lax.rem(v, pieces)
        out = jnp.dot(hbuf[v], wqkv[2], preferred_element_type=F32).astype(BF16)
        for d in range(2):
            src = chip(-s) if d == 0 else chip(s)
            for cc in range(2):
                at = rows((2 * src + cc) * n_rows + d * half + p * PIECE, PIECE)
                lo = (2 * d + cc) * PIECE
                v_s[at, :] = out[lo:lo + PIECE]
                done = rotate(k_f[at, :] * k_gain[...], src, d, cc, p)
                for j in range(heads):
                    k_f[at, j * HEAD_DIM:(j + 1) * HEAD_DIM] = done[j]

    def drain(u):
        for d in range(2):
            pair_copy(u, d).wait_send()

            @pl.when(u < units - pieces)
            def _(d=d):
                ring_copy(u, d).wait_send()

            @pl.when((u < units - pieces) | (c != d))
            def _(d=d):
                sq_copy(u, d, 0, sib).wait_send()

    def gather_step(u, _):
        @pl.when(u >= pieces)
        def _():
            for d in range(2):
                ring_copy(u - pieces, d).wait_recv()

                @pl.when(u < units - pieces)
                def _(d=d):
                    ring_copy(u, d).start()

                pair_copy(u, d).start()

        project(u)

        @pl.when(u >= 2)
        def _():
            drain(u - 2)

        @pl.when(u < units - 1)
        def _():
            project_rest(u)

        return 0

    lax.fori_loop(0, units, gather_step, 0)
    drain(units - 2)
    drain(units - 1)

    def sq_arrived(i, _):
        peer = lax.rem(me + i, n)
        for p in range(pieces):
            remote(sq_out.at[0, 0], sq_in.at[peer, p], sq_send.at[0, 0], sq_recv.at[peer, p], sib).wait_recv()
        return 0

    lax.fori_loop(1, n, sq_arrived, 0)
    total = sq_in[0]
    for i in range(1, n):
        total = total + sq_in[i]
    inv[me] = lax.rsqrt(total / (cols * n) + EPS)

    def inv_copy(i):
        dev = lax.rem(me + i, n)
        return remote(inv.at[me], inv.at[me], iv_send.at[i], iv_recv.at[me], dev)

    def inv_start(i, _):
        inv_copy(i).start()
        return 0

    def inv_wait(i, _):
        peer = lax.rem(me + i, n)
        remote(inv.at[peer], inv.at[peer], iv_send.at[i], iv_recv.at[peer], sib).wait_recv()
        return 0

    def inv_sent(i, _):
        inv_copy(i).wait_send()
        return 0

    lax.fori_loop(1, n, inv_start, 0)
    project_rest(units - 1)

    def turn_values(i, _):
        at = rows(i * k_tile, k_tile)
        v_t[:, at] = v_s[at, :].T
        return 0

    lax.fori_loop(0, q_s.shape[0] // k_tile, turn_values, 0)
    lax.fori_loop(1, n, inv_wait, 0)
    lax.fori_loop(1, n, inv_sent, 0)

    def row_scale(which, src, d, p):
        own = lax.rem(src + (nz - 1 if d == 0 else 1), nz) * 2 + d
        return jnp.broadcast_to(inv[own, p][which:which + 1], (HEAD_DIM, HEAD_DIM)).T

    def piece_rows(src, cc, d, p):
        return rows((2 * src + cc) * n_rows + d * half + p * PIECE, PIECE)

    def finish_keys(src, _):
        for d in range(2):
            for p in range(pieces):
                scale = row_scale(1, src, d, p)
                for cc in range(2):
                    at = piece_rows(src, cc, d, p)
                    for j in range(heads):
                        lanes = slice(j * HEAD_DIM, (j + 1) * HEAD_DIM)
                        k_s[at, lanes] = (k_f[at, lanes] * scale[cc * PIECE:(cc + 1) * PIECE]).astype(BF16)
        return 0

    lax.fori_loop(0, nz, finish_keys, 0)

    scale = HEAD_DIM ** -0.5 * math.log2(math.e)

    queries = 2 * PIECE

    def attend(t, d, p):
        blk = lax.rem(z + 2 * nz - 1 - t, nz) if d == 0 else lax.rem(z + 1 + t, nz)
        factor = row_scale(0, blk, d, p)
        factor = jnp.concatenate([factor] * heads, axis=1)
        parts = []
        for cc in range(2):
            raw = q_s[piece_rows(blk, cc, d, p), :].astype(F32)
            parts.append(rotate(raw * factor[cc * PIECE:(cc + 1) * PIECE] * q_gain[...], blk, d, cc, p))
        q_t = [jnp.concatenate([parts[0][j], parts[1][j]], axis=0).T.astype(BF16) for j in range(heads)]

        def tile(at, carry, mask):
            lanes = [slice(j * HEAD_DIM, (j + 1) * HEAD_DIM) for j in range(heads)]
            score = [jnp.dot(k_s[at, lanes[j]], q_t[j], preferred_element_type=F32) for j in range(heads)]
            if mask is not None:
                score = [jnp.where(mask, sc, -1e30) for sc in score]
            peak = [jnp.maximum(carry[j][0], jnp.max(score[j], axis=0, keepdims=True)) for j in range(heads)]
            prob = [jnp.exp2(score[j] * scale - peak[j] * scale) for j in range(heads)]
            fade = [jnp.exp2((carry[j][0] - peak[j]) * scale) for j in range(heads)]
            acc = [jnp.dot(v_t[lanes[j], at], prob[j].astype(BF16), preferred_element_type=F32) for j in range(heads)]
            return tuple(
                (peak[j], carry[j][1] * fade[j] + jnp.sum(prob[j], axis=0, keepdims=True), carry[j][2] * fade[j] + acc[j])
                for j in range(heads))

        zero = (jnp.full((1, queries), -1e30, F32), jnp.zeros((1, queries), F32), jnp.zeros((HEAD_DIM, queries), F32))
        carry = lax.fori_loop(0, blk, lambda i, kept: tile(rows(i * k_tile, k_tile), kept, None), (zero,) * heads)
        key = lax.broadcasted_iota(jnp.int32, (k_tile, queries), 0)
        r = lax.broadcasted_iota(jnp.int32, (k_tile, queries), 1)
        mask = jnp.where(r < PIECE, r, r + (n_rows - PIECE)) + (d * half + p * PIECE) >= key
        carry = tile(rows(blk * k_tile, k_tile), carry, mask)
        for j in range(heads):
            _, l, acc = carry[j]
            o_s[:, j * HEAD_DIM:(j + 1) * HEAD_DIM] = (acc / l).T.astype(BF16)

    def share_copy(t, d, p):
        return remote(
            ybuf.at[1, d, pl.ds(p * PIECE, PIECE)], hbuf.at[shares + t, pl.ds(d * half + p * PIECE, PIECE)],
            sb_send.at[t, d * pieces + p], sb_recv.at[t, d * pieces + p], sib)

    y_tile = min(width, 1024)

    def emit(t, d, p):
        @pl.when(t >= 1)
        def _():
            share_copy(t - 1, d, p).wait_send()

        def column(i, _):
            at = rows(i * y_tile, y_tile)
            y = jnp.dot(o_s[...], wo[:, at], preferred_element_type=F32).astype(BF16)
            for cc in range(2):
                ybuf[cc + c - 2 * cc * c, d, pl.ds(p * PIECE, PIECE), at] = y[cc * PIECE:(cc + 1) * PIECE]
            return 0

        lax.fori_loop(0, width // y_tile, column, 0)
        share_copy(t, d, p).start()

    def sum_copy(s, d, k):
        at = rows(d * half + k * sub, sub)
        return remote(hbuf.at[s, at], hbuf.at[s + 1, at], rs_send.at[s, d * SUM_PIECES + k],
                      rs_recv.at[s, d * SUM_PIECES + k], toward(d) * 2 + c)

    def out_copy(d, k):
        at = rows(d * half + k * sub, sub)
        return pltpu.make_async_copy(hbuf.at[nz - 1, at], out_hbm.at[at], out_sem.at[d * SUM_PIECES + k])

    def add_up(s, k):
        for d in range(2):
            if k * sub % PIECE == 0:
                share_copy(s, d, k * sub // PIECE).wait_recv()

            @pl.when(s >= 1)
            def _(d=d):
                sum_copy(s - 1, d, k).wait_recv()

            at = rows(d * half + k * sub, sub)

            def column(i, _, d=d, at=at):
                lanes = rows(i * y_tile, y_tile)
                y = ybuf[0, d, pl.ds(k * sub, sub), lanes].astype(F32)
                y = y + hbuf[shares + s, at, lanes].astype(F32)
                run = hbuf[s, at, lanes].astype(F32)
                y = (y + jnp.where(s >= 1, run, 0.0)).astype(BF16)
                hbuf[s, at, lanes] = y

                @pl.when(s == nz - 1)
                def _():
                    hbuf[s, at, lanes] = (hbuf[shares, at, lanes].astype(F32) + y.astype(F32)).astype(BF16)

                return 0

            lax.fori_loop(0, width // y_tile, column, 0)

            @pl.when(s < nz - 1)
            def _(d=d):
                sum_copy(s, d, k).start()

            @pl.when(s == nz - 1)
            def _(d=d):
                out_copy(d, k).start()

    x_again = pltpu.make_async_copy(x_hbm, hbuf.at[shares], ld_sem.at[0])

    def cache_copy(i, which):
        at = rows(i * cast_rows, cast_rows)
        return pltpu.make_async_copy(
            kv_st.at[which, lax.rem(i, 2)], (k_hbm, v_hbm)[which].at[at], st_sem.at[which, lax.rem(i, 2)])

    def write_caches(i):
        for which in range(2):
            @pl.when(i >= 2)
            def _(which=which):
                cache_copy(i - 2, which).wait()

            part = (k_s, v_s)[which][rows(i * cast_rows, cast_rows), :]
            kv_st[which, lax.rem(i, 2)] = part.reshape(cast_rows, heads, HEAD_DIM)
            cache_copy(i, which).start()

    def scatter_step(t, _):
        @pl.when(t == 2)
        def _():
            x_again.start()

        @pl.when(t == nz)
        def _():
            x_again.wait()

        for k in range(SUM_PIECES):
            @pl.when(t >= 1)
            def _(k=k):
                write_caches((t - 1) * SUM_PIECES + k)
                add_up(t - 1, k)

            d, late = k % 2, k < 2

            @pl.when((t >= 1) if late else (t < nz))
            def _(d=d, late=late):
                attend(t - late, d, int(late))
                emit(t - late, d, int(late))

        return 0

    lax.fori_loop(0, nz + 1, scatter_step, 0)

    def drain_scatter(s, _):
        for d in range(2):
            for k in range(SUM_PIECES):
                sum_copy(s, d, k).wait_send()
        return 0

    lax.fori_loop(0, nz - 1, drain_scatter, 0)
    for d in range(2):
        for p in range(pieces):
            share_copy(nz - 1, d, p).wait_send()
        for k in range(SUM_PIECES):
            out_copy(d, k).wait()
    for i in (nz * SUM_PIECES - 2, nz * SUM_PIECES - 1):
        for which in range(2):
            cache_copy(i, which).wait()


def solution(mesh):
    n = mesh.shape["tp"]

    def local_block(x_local, attn_gain, wq, wk, wv, q_gain, k_gain, wo):
        _, n_rows, width = x_local.shape
        cols = wq.shape[1]
        seq_len = n * n_rows
        nz, pieces = n // 2, n_rows // 2 // PIECE
        units = nz * pieces
        tables = rope_constants(seq_len)
        any_spec = pl.BlockSpec(memory_space=pl.ANY)
        vmem_spec = pl.BlockSpec(memory_space=pltpu.VMEM)
        dma = pltpu.SemaphoreType.DMA
        out, k_rot, v_rows = pl.pallas_call(
            functools.partial(block_kernel, n),
            out_shape=(
                jax.ShapeDtypeStruct((n_rows, width), BF16),
                jax.ShapeDtypeStruct((seq_len, cols // HEAD_DIM, HEAD_DIM), BF16),
                jax.ShapeDtypeStruct((seq_len, cols // HEAD_DIM, HEAD_DIM), BF16),
            ),
            in_specs=[any_spec, vmem_spec] + [any_spec] * 4 + [vmem_spec] * 6,
            out_specs=(any_spec,) * 3,
            scratch_shapes=[
                pltpu.VMEM((units, 4 * PIECE, width), BF16),
                pltpu.VMEM((3, width, cols), BF16),
                pltpu.VMEM((cols, width), BF16),
                pltpu.VMEM((seq_len, cols), BF16),
                pltpu.VMEM((seq_len, cols), F32),
                pltpu.VMEM((seq_len, cols), BF16),
                pltpu.VMEM((seq_len, cols), BF16),
                pltpu.VMEM((cols, seq_len), BF16),
                pltpu.VMEM((2, 2, n_rows // 2, width), BF16),
                pltpu.VMEM((2 * PIECE, cols), BF16),
                pltpu.VMEM((2, 2, seq_len // (nz * SUM_PIECES), cols // HEAD_DIM, HEAD_DIM), BF16),
                pltpu.VMEM((units, 2, 2, 2 * PIECE), F32),
                pltpu.VMEM((n, pieces, 2, 2 * PIECE), F32),
                pltpu.VMEM((n, pieces, 2, 2 * PIECE), F32),
                dma((4 + 2 * pieces,)),
                dma((units, 2)), dma((units, 2)), dma((units, 2)), dma((units, 2)),
                dma((units, 2)), dma((n, pieces)), dma((n,)), dma((n,)),
                dma((nz - 1, 2 * SUM_PIECES)), dma((nz - 1, 2 * SUM_PIECES)),
                dma((nz, 2 * pieces)), dma((nz, 2 * pieces)), dma((2, 2)), dma((2 * SUM_PIECES,)),
            ],
            compiler_params=pltpu.CompilerParams(
                collective_id=0, has_side_effects=True, vmem_limit_bytes=67043328),
            name="attention_block",
        )(x_local[0], attn_gain[None], wq, wk, wv, wo, q_gain[None], k_gain[None], *tables)
        return out[None], k_rot[None], v_rows[None]

    seq_spec = P("dp", "tp", None)
    head_spec = P("dp", None, "tp", None)
    col_spec = P(None, "tp")
    return jax.shard_map(
        local_block, mesh=mesh,
        in_specs=(seq_spec, P(None), col_spec, col_spec, col_spec, P("tp"), P("tp"), P("tp", None)),
        out_specs=(seq_spec, head_spec, head_spec), check_vma=False)
```

time: 374 us -> 362 us (0.968)
  Pallas kernels: 363 us -> 354 us
    pallas_call x1, Pallas kernels: 363 us -> 354 us  [local_block(): pl.pallas_call(functools.partial(block_kernel, n), out_shape=(jax.ShapeDt...]
    reshape x2 -> x0, local copies, waits for them, and re-layouts: 8.06 us -> none  [local_block(): return (out[None], k_rot.reshape(head_shape), v_rows.reshape(head_shape))]
    unnamed x3 -> x7, local copies, waits for them, and re-layouts: 1.32 us -> 6.95 us
where the time goes in v2:
time: 362 us
  Pallas kernels  354 us (98%)
  local copies, waits for them, and re-layouts  6.95 us (2%)
    pallas_call x1, Pallas kernels, local_block(): pl.pallas_call(functools.partial(block_kernel, n), out_shape=(jax.ShapeDt...  354 us

profile of v2, /device:TPU:21, one launch (start us, length us, event | category | flops | bytes accessed | tf_op | source)
XLA Modules:
  0.0 361.5 jit_solution(2744251483184207917)
XLA Ops:
  0.6 353.9 %attention_block.1 = (bf16[256,4096]{1,0:T(8,128)(2,1)}, bf16[4096,2,128]{2,1,0:T(2,128)(2,1)}, bf16[4096,2,128]{2,1,0:T(2,128)(2,1)}) custom-call(bf16[256,4096]{1,0:T(8,128)(2,1)} %bitcast.10, f32[1,4096]{1,0:T(1,128)} %bitcast.11, bf16[4096,256]{1,0:T(8,128)(2,1)} %wq_hbm.1, bf16[4096,256]{1,0:T(8,128)(2,1)} %wk_hbm.1, bf16[4096,256]{1,0:T(8,128)(2,1)} %wv_hbm.1, ...), custom_call_target="tpu_custom_call" | custom-call | tf_op jit(solution)/shard_map/attention_block/pallas_call | solution.py:455
  354.5 0.0 copy-start.1
  354.6 3.3 copy.18
  357.8 0.0 copy-done.1
  357.8 0.0 copy-start
  357.8 1.3 copy.19
  359.2 1.0 copy-done
  360.2 1.3 copy.20
Async XLA Ops:
  354.5 3.3 copy-start.1
  357.8 2.3 copy-start

commit v3 on v2

--- a/solution.py
+++ b/solution.py
@@ -13,6 +13,8 @@
 EPS = 1e-5
 PIECE = 64
 SUM_PIECES = 4
+KERNEL_VMEM = 60700000
+FLUSH_PARTS = 4
 F32 = jnp.float32
 BF16 = jnp.bfloat16
 
@@ -30,7 +32,7 @@
 def block_kernel(
     n, x_hbm, gain, wq_hbm, wk_hbm, wv_hbm, wo_hbm, q_gain, k_gain, cos_b, sin_b, cos_o, sin_o,
     out_hbm, k_hbm, v_hbm,
-    hbuf, wqkv, wo, q_s, k_f, k_s, v_s, v_t, ybuf, o_s, kv_st, sq_out, sq_in, inv,
+    hbuf, wqkv, wo, q_s, k_f, v_s, v_t, ybuf, o_s, kv_st, sq_out, sq_in, sums,
     ld_sem, ag_send, ag_recv, dd_send, dd_recv, sq_send, sq_recv, iv_send, iv_recv,
     rs_send, rs_recv, sb_send, sb_recv, st_sem, out_sem,
 ):
@@ -49,6 +51,8 @@
     shares = units // 2
     cast_rows = q_s.shape[0] // (nz * SUM_PIECES)
 
+    k_s = wqkv.at[0]
+
     def chip(offset):
         return lax.rem(z + offset + 2 * nz, nz)
 
@@ -63,6 +67,9 @@
             src_ref=src, dst_ref=dst, send_sem=send, recv_sem=recv,
             device_id={"tp": dev}, device_id_type=pl.DeviceIdType.MESH)
 
+    def wait_bytes(ref, sem):
+        remote(ref, ref, sem, sem, sib).wait_recv()
+
     def x_load(d, p):
         at = pl.ds(d * half + p * PIECE, PIECE)
         return pltpu.make_async_copy(x_hbm.at[at], ybuf.at[0, d, pl.ds(p * PIECE, PIECE)], ld_sem.at[4 + d * pieces + p])
@@ -70,7 +77,7 @@
     for p in range(pieces):
         for d in range(2):
             x_load(d, p).start()
-    loads = [pltpu.make_async_copy(w, wqkv.at[i], ld_sem.at[i]) for i, w in enumerate((wq_hbm, wk_hbm, wv_hbm))]
+    loads = [pltpu.make_async_copy(w, wqkv.at[i, pl.ds(0, width)], ld_sem.at[i]) for i, w in enumerate((wq_hbm, wk_hbm, wv_hbm))]
     loads.append(pltpu.make_async_copy(wo_hbm, wo, ld_sem.at[3]))
 
     barrier = pltpu.get_barrier_semaphore()
@@ -85,10 +92,10 @@
         return hbuf.at[u, rows((2 * d + c) * PIECE, PIECE)]
 
     def ring_copy(u, d):
-        return remote(quarter(u, d), quarter(u + pieces, d), ag_send.at[u, d], ag_recv.at[u, d], toward(d) * 2 + c)
+        return remote(quarter(u, d), quarter(u + pieces, d), ag_send.at[lax.rem(u, 4), d], ag_recv.at[u], toward(d) * 2 + c)
 
     def pair_copy(u, d):
-        return remote(quarter(u, d), quarter(u, d), dd_send.at[u, d], dd_recv.at[u, d], sib)
+        return remote(quarter(u, d), quarter(u, d), dd_send.at[lax.rem(u, 4), d], dd_recv.at[u], sib)
 
     for p in range(pieces):
         for d in range(2):
@@ -105,7 +112,7 @@
             pair_copy(p, d).start()
 
     def sq_copy(u, d, p, dev):
-        return remote(sq_out.at[u, d], sq_in.at[me, p], sq_send.at[u, d], sq_recv.at[me, p], dev)
+        return remote(sq_out.at[u, d], sq_in.at[z, d, p], sq_send.at[lax.rem(u, 4), d], sq_recv, dev)
 
     def rotate(t, src, d, cc, p):
         b = (2 * src + cc) * (n_rows // PIECE) + d * pieces + p
@@ -117,8 +124,7 @@
 
     def project(v):
         s, p = v // pieces, lax.rem(v, pieces)
-        for d in range(2):
-            pair_copy(v, d).wait_recv()
+        wait_bytes(hbuf.at[v, pl.ds(0, 2 * PIECE)], dd_recv.at[v])
 
         @pl.when(v == 0)
         def _():
@@ -131,40 +137,36 @@
         def at(d, cc, src):
             return rows((2 * src + cc) * n_rows + d * half + p * PIECE, PIECE)
 
-        outs, sums = [], []
+        outs, squares = [], []
         for i in range(2):
-            out = jnp.dot(h, wqkv[i], preferred_element_type=F32).astype(BF16)
+            out = jnp.dot(h, wqkv[i, :width], preferred_element_type=F32).astype(BF16)
             wide = out.astype(F32)
             sq = wide * wide
             lanes = sq[:, :HEAD_DIM]
             for j in range(1, heads):
                 lanes = lanes + sq[:, j * HEAD_DIM:(j + 1) * HEAD_DIM]
             outs.append(out)
-            sums.append(lanes)
+            squares.append(lanes)
         for d, cc, src, lo in parts:
             q_s[at(d, cc, src), :] = outs[0][lo:lo + PIECE]
             k_f[at(d, cc, src), :] = outs[1][lo:lo + PIECE].astype(F32)
         for d in range(2):
             for i in range(2):
-                part = sums[i][d * 2 * PIECE:(d + 1) * 2 * PIECE]
+                part = squares[i][d * 2 * PIECE:(d + 1) * 2 * PIECE]
                 sq_out[v, d, pl.ds(i, 1), :] = jnp.sum(part.T, axis=0, keepdims=True)
             owner = chip(-s - 1) if d == 0 else chip(s + 1)
 
             @pl.when(s < nz - 1)
             def _(d=d, owner=owner):
-                sq_copy(v, d, p, owner * 2 + d).start()
-
-            @pl.when((s == nz - 1) & (c != d))
+                sq_copy(v, d, p, owner * 2 + c).start()
+
+            @pl.when(s == nz - 1)
             def _(d=d):
-                sq_copy(v, d, p, sib).start()
-
-            @pl.when((s == nz - 1) & (c == d))
-            def _(d=d):
-                sq_in[me, p] = sq_out[v, d]
+                sq_in[z, d, p] = sq_out[v, d]
 
     def project_rest(v):
         s, p = v // pieces, lax.rem(v, pieces)
-        out = jnp.dot(hbuf[v], wqkv[2], preferred_element_type=F32).astype(BF16)
+        out = jnp.dot(hbuf[v], wqkv[2, :width], preferred_element_type=F32).astype(BF16)
         for d in range(2):
             src = chip(-s) if d == 0 else chip(s)
             for cc in range(2):
@@ -182,17 +184,13 @@
             @pl.when(u < units - pieces)
             def _(d=d):
                 ring_copy(u, d).wait_send()
-
-            @pl.when((u < units - pieces) | (c != d))
-            def _(d=d):
                 sq_copy(u, d, 0, sib).wait_send()
 
     def gather_step(u, _):
         @pl.when(u >= pieces)
         def _():
+            wait_bytes(hbuf.at[u, pl.ds(0, 2 * PIECE)], ag_recv.at[u - pieces])
             for d in range(2):
-                ring_copy(u - pieces, d).wait_recv()
-
                 @pl.when(u < units - pieces)
                 def _(d=d):
                     ring_copy(u, d).start()
@@ -215,33 +213,18 @@
     drain(units - 2)
     drain(units - 1)
 
-    def sq_arrived(i, _):
-        peer = lax.rem(me + i, n)
-        for p in range(pieces):
-            remote(sq_out.at[0, 0], sq_in.at[peer, p], sq_send.at[0, 0], sq_recv.at[peer, p], sib).wait_recv()
-        return 0
-
-    lax.fori_loop(1, n, sq_arrived, 0)
+    wait_bytes(sq_in.at[pl.ds(0, nz - 1)], sq_recv)
     total = sq_in[0]
-    for i in range(1, n):
+    for i in range(1, nz):
         total = total + sq_in[i]
-    inv[me] = lax.rsqrt(total / (cols * n) + EPS)
+    sums[me] = total
 
     def inv_copy(i):
         dev = lax.rem(me + i, n)
-        return remote(inv.at[me], inv.at[me], iv_send.at[i], iv_recv.at[me], dev)
+        return remote(sums.at[me], sums.at[me], iv_send, iv_recv, dev)
 
     def inv_start(i, _):
         inv_copy(i).start()
-        return 0
-
-    def inv_wait(i, _):
-        peer = lax.rem(me + i, n)
-        remote(inv.at[peer], inv.at[peer], iv_send.at[i], iv_recv.at[peer], sib).wait_recv()
-        return 0
-
-    def inv_sent(i, _):
-        inv_copy(i).wait_send()
         return 0
 
     lax.fori_loop(1, n, inv_start, 0)
@@ -253,12 +236,14 @@
         return 0
 
     lax.fori_loop(0, q_s.shape[0] // k_tile, turn_values, 0)
-    lax.fori_loop(1, n, inv_wait, 0)
-    lax.fori_loop(1, n, inv_sent, 0)
+    others = sums.at[pl.ds(0, n - 1)]
+    wait_bytes(others, iv_recv)
+    remote(others, others, iv_send, iv_recv, sib).wait_send()
 
     def row_scale(which, src, d, p):
-        own = lax.rem(src + (nz - 1 if d == 0 else 1), nz) * 2 + d
-        return jnp.broadcast_to(inv[own, p][which:which + 1], (HEAD_DIM, HEAD_DIM)).T
+        own = lax.rem(src + (nz - 1 if d == 0 else 1), nz) * 2
+        total = sums[own, d, p][which:which + 1] + sums[own + 1, d, p][which:which + 1]
+        return jnp.broadcast_to(lax.rsqrt(total / (cols * n) + EPS), (HEAD_DIM, HEAD_DIM)).T
 
     def piece_rows(src, cc, d, p):
         return rows((2 * src + cc) * n_rows + d * half + p * PIECE, PIECE)
@@ -316,9 +301,9 @@
     def share_copy(t, d, p):
         return remote(
             ybuf.at[1, d, pl.ds(p * PIECE, PIECE)], hbuf.at[shares + t, pl.ds(d * half + p * PIECE, PIECE)],
-            sb_send.at[t, d * pieces + p], sb_recv.at[t, d * pieces + p], sib)
-
-    y_tile = min(width, 1024)
+            sb_send.at[d * pieces + p], sb_recv.at[t, p], sib)
+
+    y_tile, e_tile = min(width, 1024), min(width, 2048)
 
     def emit(t, d, p):
         @pl.when(t >= 1)
@@ -326,33 +311,33 @@
             share_copy(t - 1, d, p).wait_send()
 
         def column(i, _):
-            at = rows(i * y_tile, y_tile)
+            at = rows(i * e_tile, e_tile)
             y = jnp.dot(o_s[...], wo[:, at], preferred_element_type=F32).astype(BF16)
             for cc in range(2):
                 ybuf[cc + c - 2 * cc * c, d, pl.ds(p * PIECE, PIECE), at] = y[cc * PIECE:(cc + 1) * PIECE]
             return 0
 
-        lax.fori_loop(0, width // y_tile, column, 0)
+        lax.fori_loop(0, width // e_tile, column, 0)
         share_copy(t, d, p).start()
 
     def sum_copy(s, d, k):
         at = rows(d * half + k * sub, sub)
-        return remote(hbuf.at[s, at], hbuf.at[s + 1, at], rs_send.at[s, d * SUM_PIECES + k],
-                      rs_recv.at[s, d * SUM_PIECES + k], toward(d) * 2 + c)
+        return remote(hbuf.at[s, at], hbuf.at[s + 1, at], rs_send.at[d * SUM_PIECES + k],
+                      rs_recv.at[s, k], toward(d) * 2 + c)
 
     def out_copy(d, k):
         at = rows(d * half + k * sub, sub)
         return pltpu.make_async_copy(hbuf.at[nz - 1, at], out_hbm.at[at], out_sem.at[d * SUM_PIECES + k])
 
     def add_up(s, k):
-        for d in range(2):
-            if k * sub % PIECE == 0:
-                share_copy(s, d, k * sub // PIECE).wait_recv()
-
-            @pl.when(s >= 1)
-            def _(d=d):
-                sum_copy(s - 1, d, k).wait_recv()
-
+        if k * sub % PIECE == 0:
+            wait_bytes(hbuf.at[shares + s, pl.ds(0, 2 * PIECE)], sb_recv.at[s, k * sub // PIECE])
+
+        @pl.when(s >= 1)
+        def _():
+            wait_bytes(hbuf.at[s, pl.ds(0, 2 * sub)], rs_recv.at[s - 1, k])
+
+        for d in range(2):
             at = rows(d * half + k * sub, sub)
 
             def column(i, _, d=d, at=at):
@@ -371,6 +356,10 @@
 
             lax.fori_loop(0, width // y_tile, column, 0)
 
+            @pl.when(s >= 1)
+            def _(d=d):
+                sum_copy(s - 1, d, k).wait_send()
+
             @pl.when(s < nz - 1)
             def _(d=d):
                 sum_copy(s, d, k).start()
@@ -422,13 +411,6 @@
 
     lax.fori_loop(0, nz + 1, scatter_step, 0)
 
-    def drain_scatter(s, _):
-        for d in range(2):
-            for k in range(SUM_PIECES):
-                sum_copy(s, d, k).wait_send()
-        return 0
-
-    lax.fori_loop(0, nz - 1, drain_scatter, 0)
     for d in range(2):
         for p in range(pieces):
             share_copy(nz - 1, d, p).wait_send()
@@ -439,6 +421,19 @@
             cache_copy(i, which).wait()
 
 
+def flush_kernel(out_ref, k_ref, v_ref, out_hbm, k_hbm, v_hbm, sem):
+    copies = []
+    for i, (src, dst) in enumerate(((out_ref, out_hbm), (k_ref, k_hbm), (v_ref, v_hbm))):
+        part = src.shape[0] // FLUSH_PARTS
+        for j in range(FLUSH_PARTS):
+            at = pl.ds(j * part, part)
+            copies.append(pltpu.make_async_copy(src.at[at], dst.at[at], sem.at[i, j]))
+    for copy in copies:
+        copy.start()
+    for copy in copies:
+        copy.wait()
+
+
 def solution(mesh):
     n = mesh.shape["tp"]
 
@@ -449,43 +444,47 @@
         nz, pieces = n // 2, n_rows // 2 // PIECE
         units = nz * pieces
         tables = rope_constants(seq_len)
+        shapes = ((n_rows, width),) + ((seq_len, cols // HEAD_DIM, HEAD_DIM),) * 2
         any_spec = pl.BlockSpec(memory_space=pl.ANY)
         vmem_spec = pl.BlockSpec(memory_space=pltpu.VMEM)
         dma = pltpu.SemaphoreType.DMA
-        out, k_rot, v_rows = pl.pallas_call(
+        held = pl.pallas_call(
             functools.partial(block_kernel, n),
-            out_shape=(
-                jax.ShapeDtypeStruct((n_rows, width), BF16),
-                jax.ShapeDtypeStruct((seq_len, cols // HEAD_DIM, HEAD_DIM), BF16),
-                jax.ShapeDtypeStruct((seq_len, cols // HEAD_DIM, HEAD_DIM), BF16),
-            ),
+            out_shape=tuple(pltpu.VMEM(shape, BF16) for shape in shapes),
             in_specs=[any_spec, vmem_spec] + [any_spec] * 4 + [vmem_spec] * 6,
             out_specs=(any_spec,) * 3,
             scratch_shapes=[
                 pltpu.VMEM((units, 4 * PIECE, width), BF16),
-                pltpu.VMEM((3, width, cols), BF16),
+                pltpu.VMEM((3, max(width, seq_len), cols), BF16),
                 pltpu.VMEM((cols, width), BF16),
                 pltpu.VMEM((seq_len, cols), BF16),
                 pltpu.VMEM((seq_len, cols), F32),
-                pltpu.VMEM((seq_len, cols), BF16),
                 pltpu.VMEM((seq_len, cols), BF16),
                 pltpu.VMEM((cols, seq_len), BF16),
                 pltpu.VMEM((2, 2, n_rows // 2, width), BF16),
                 pltpu.VMEM((2 * PIECE, cols), BF16),
                 pltpu.VMEM((2, 2, seq_len // (nz * SUM_PIECES), cols // HEAD_DIM, HEAD_DIM), BF16),
                 pltpu.VMEM((units, 2, 2, 2 * PIECE), F32),
-                pltpu.VMEM((n, pieces, 2, 2 * PIECE), F32),
-                pltpu.VMEM((n, pieces, 2, 2 * PIECE), F32),
+                pltpu.VMEM((nz, 2, pieces, 2, 2 * PIECE), F32),
+                pltpu.VMEM((n, 2, pieces, 2, 2 * PIECE), F32),
                 dma((4 + 2 * pieces,)),
-                dma((units, 2)), dma((units, 2)), dma((units, 2)), dma((units, 2)),
-                dma((units, 2)), dma((n, pieces)), dma((n,)), dma((n,)),
-                dma((nz - 1, 2 * SUM_PIECES)), dma((nz - 1, 2 * SUM_PIECES)),
-                dma((nz, 2 * pieces)), dma((nz, 2 * pieces)), dma((2, 2)), dma((2 * SUM_PIECES,)),
+                dma((4, 2)), dma((units,)), dma((4, 2)), dma((units,)),
+                dma((4, 2)), dma, dma, dma,
+                dma((2 * SUM_PIECES,)), dma((nz - 1, SUM_PIECES)),
+                dma((2 * pieces,)), dma((nz, pieces)), dma((2, 2)), dma((2 * SUM_PIECES,)),
             ],
             compiler_params=pltpu.CompilerParams(
-                collective_id=0, has_side_effects=True, vmem_limit_bytes=67043328),
+                collective_id=0, has_side_effects=True, vmem_limit_bytes=KERNEL_VMEM),
             name="attention_block",
         )(x_local[0], attn_gain[None], wq, wk, wv, wo, q_gain[None], k_gain[None], *tables)
+        out, k_rot, v_rows = pl.pallas_call(
+            flush_kernel,
+            out_shape=tuple(jax.ShapeDtypeStruct(shape, BF16) for shape in shapes),
+            in_specs=[any_spec] * 3, out_specs=(any_spec,) * 3,
+            scratch_shapes=[dma((3, FLUSH_PARTS))],
+            compiler_params=pltpu.CompilerParams(vmem_limit_bytes=1 << 18),
+            name="write_out",
+        )(*held)
         return out[None], k_rot[None], v_rows[None]
 
     seq_spec = P("dp", "tp", None)

time: 362 us -> 353 us (0.975)
  local copies, waits for them, and re-layouts: 6.95 us -> 0 us
    unnamed x7 -> x0, local copies, waits for them, and re-layouts: 6.95 us -> none
    pallas_call x1 -> x2, Pallas kernels: 354 us -> 352 us  [the longest x1 350 us: local_block(): pl.pallas_call(functools.partial(block_kernel, n), out_shape=tuple((pltpu...]
where the time goes in v3:
time: 353 us
  Pallas kernels  352 us (100%)
    pallas_call x1, Pallas kernels, local_block(): pl.pallas_call(functools.partial(block_kernel, n), out_shape=tuple((pltpu...  350 us

profile of v3, /device:TPU:21, one launch (start us, length us, event | category | flops | bytes accessed | tf_op | source)
XLA Modules:
  0.0 353.0 jit_solution(14164035641825573494)
XLA Ops:
  0.6 349.6 %attention_block.1 = (bf16[256,4096]{1,0:T(8,128)(2,1)S(1)}, bf16[4096,2,128]{2,1,0:T(2,128)(2,1)S(1)}, bf16[4096,2,128]{2,1,0:T(2,128)(2,1)S(1)}) custom-call(bf16[256,4096]{1,0:T(8,128)(2,1)} %bitcast.7, f32[1,4096]{1,0:T(1,128)} %bitcast.8, bf16[4096,256]{1,0:T(8,128)(2,1)} %wq_hbm.1, bf16[4096,256]{1,0:T(8,128)(2,1)} %wk_hbm.1, ...), custom_call_target="tpu_custom_call" | custom-call | tf_op jit(solution)/shard_map/attention_block/pallas_call | solution.py:451
  350.2 2.8 write_out.1

commit v4 on v3

--- a/solution.py
+++ b/solution.py
@@ -82,11 +82,8 @@
 
     barrier = pltpu.get_barrier_semaphore()
 
-    def greet(i, _):
-        pl.semaphore_signal(barrier, inc=1, device_id={"tp": lax.rem(me + i, n)}, device_id_type=pl.DeviceIdType.MESH)
-        return 0
-
-    lax.fori_loop(1, n, greet, 0)
+    for dev in (sib, toward(0) * 2 + c, toward(1) * 2 + c):
+        pl.semaphore_signal(barrier, inc=1, device_id={"tp": dev}, device_id_type=pl.DeviceIdType.MESH)
 
     def quarter(u, d):
         return hbuf.at[u, rows((2 * d + c) * PIECE, PIECE)]
@@ -106,7 +103,7 @@
         if p == 0:
             for load in loads:
                 load.start()
-            pl.semaphore_wait(barrier, n - 1)
+            pl.semaphore_wait(barrier, 3)
         for d in range(2):
             ring_copy(p, d).start()
             pair_copy(p, d).start()
@@ -275,25 +272,38 @@
             parts.append(rotate(raw * factor[cc * PIECE:(cc + 1) * PIECE] * q_gain[...], blk, d, cc, p))
         q_t = [jnp.concatenate([parts[0][j], parts[1][j]], axis=0).T.astype(BF16) for j in range(heads)]
 
-        def tile(at, carry, mask):
-            lanes = [slice(j * HEAD_DIM, (j + 1) * HEAD_DIM) for j in range(heads)]
-            score = [jnp.dot(k_s[at, lanes[j]], q_t[j], preferred_element_type=F32) for j in range(heads)]
-            if mask is not None:
-                score = [jnp.where(mask, sc, -1e30) for sc in score]
+        head = [slice(j * HEAD_DIM, (j + 1) * HEAD_DIM) for j in range(heads)]
+
+        def scores(at):
+            return [jnp.dot(k_s[at, head[j]], q_t[j], preferred_element_type=F32) for j in range(heads)]
+
+        def update(at, score, carry):
             peak = [jnp.maximum(carry[j][0], jnp.max(score[j], axis=0, keepdims=True)) for j in range(heads)]
             prob = [jnp.exp2(score[j] * scale - peak[j] * scale) for j in range(heads)]
             fade = [jnp.exp2((carry[j][0] - peak[j]) * scale) for j in range(heads)]
-            acc = [jnp.dot(v_t[lanes[j], at], prob[j].astype(BF16), preferred_element_type=F32) for j in range(heads)]
+            acc = [jnp.dot(v_t[head[j], at], prob[j].astype(BF16), preferred_element_type=F32) for j in range(heads)]
             return tuple(
                 (peak[j], carry[j][1] * fade[j] + jnp.sum(prob[j], axis=0, keepdims=True), carry[j][2] * fade[j] + acc[j])
                 for j in range(heads))
 
+        def one(i, carry):
+            at = rows(i * k_tile, k_tile)
+            return update(at, scores(at), carry)
+
+        def two(i, carry):
+            at = [rows((2 * i + m) * k_tile, k_tile) for m in range(2)]
+            both = [scores(a) for a in at]
+            return update(at[1], both[1], update(at[0], both[0], carry))
+
         zero = (jnp.full((1, queries), -1e30, F32), jnp.zeros((1, queries), F32), jnp.zeros((HEAD_DIM, queries), F32))
-        carry = lax.fori_loop(0, blk, lambda i, kept: tile(rows(i * k_tile, k_tile), kept, None), (zero,) * heads)
+        pairs = blk // 2
+        carry = lax.fori_loop(0, pairs, two, (zero,) * heads)
+        carry = lax.fori_loop(2 * pairs, blk, one, carry)
         key = lax.broadcasted_iota(jnp.int32, (k_tile, queries), 0)
         r = lax.broadcasted_iota(jnp.int32, (k_tile, queries), 1)
         mask = jnp.where(r < PIECE, r, r + (n_rows - PIECE)) + (d * half + p * PIECE) >= key
-        carry = tile(rows(blk * k_tile, k_tile), carry, mask)
+        at = rows(blk * k_tile, k_tile)
+        carry = update(at, [jnp.where(mask, sc, -1e30) for sc in scores(at)], carry)
         for j in range(heads):
             _, l, acc = carry[j]
             o_s[:, j * HEAD_DIM:(j + 1) * HEAD_DIM] = (acc / l).T.astype(BF16)

time: 353 us -> 351 us (level)
  no operation moved by 1% of the time
where the time goes in v4:
time: 351 us; the launch traced here: 350 us
  Pallas kernels  350 us (100%)
    pallas_call x1, Pallas kernels, local_block(): pl.pallas_call(functools.partial(block_kernel, n), out_shape=tuple((pltpu...  347 us

profile of v4, /device:TPU:21, one launch (start us, length us, event | category | flops | bytes accessed | tf_op | source)
XLA Modules:
  0.0 350.4 jit_solution(10079336120037284855)
XLA Ops:
  0.6 347.0 %attention_block.1 = (bf16[256,4096]{1,0:T(8,128)(2,1)S(1)}, bf16[4096,2,128]{2,1,0:T(2,128)(2,1)S(1)}, bf16[4096,2,128]{2,1,0:T(2,128)(2,1)S(1)}) custom-call(bf16[256,4096]{1,0:T(8,128)(2,1)} %bitcast.7, f32[1,4096]{1,0:T(1,128)} %bitcast.8, bf16[4096,256]{1,0:T(8,128)(2,1)} %wq_hbm.1, bf16[4096,256]{1,0:T(8,128)(2,1)} %wk_hbm.1, ...), custom_call_target="tpu_custom_call" | custom-call | tf_op jit(solution)/shard_map/attention_block/pallas_call | solution.py:461
  347.6 2.8 write_out.1

commit v5 on v4

--- a/solution.py
+++ b/solution.py
@@ -89,10 +89,10 @@
         return hbuf.at[u, rows((2 * d + c) * PIECE, PIECE)]
 
     def ring_copy(u, d):
-        return remote(quarter(u, d), quarter(u + pieces, d), ag_send.at[lax.rem(u, 4), d], ag_recv.at[u], toward(d) * 2 + c)
+        return remote(quarter(u, d), quarter(u + pieces, d), ag_send.at[lax.rem(u, 4)], ag_recv.at[u], toward(d) * 2 + c)
 
     def pair_copy(u, d):
-        return remote(quarter(u, d), quarter(u, d), dd_send.at[lax.rem(u, 4), d], dd_recv.at[u], sib)
+        return remote(quarter(u, d), quarter(u, d), dd_send.at[lax.rem(u, 4)], dd_recv.at[u], sib)
 
     for p in range(pieces):
         for d in range(2):
@@ -109,7 +109,7 @@
             pair_copy(p, d).start()
 
     def sq_copy(u, d, p, dev):
-        return remote(sq_out.at[u, d], sq_in.at[z, d, p], sq_send.at[lax.rem(u, 4), d], sq_recv, dev)
+        return remote(sq_out.at[u, d], sq_in.at[z, d, p], sq_send.at[lax.rem(u, 4)], sq_recv, dev)
 
     def rotate(t, src, d, cc, p):
         b = (2 * src + cc) * (n_rows // PIECE) + d * pieces + p
@@ -144,9 +144,6 @@
                 lanes = lanes + sq[:, j * HEAD_DIM:(j + 1) * HEAD_DIM]
             outs.append(out)
             squares.append(lanes)
-        for d, cc, src, lo in parts:
-            q_s[at(d, cc, src), :] = outs[0][lo:lo + PIECE]
-            k_f[at(d, cc, src), :] = outs[1][lo:lo + PIECE].astype(F32)
         for d in range(2):
             for i in range(2):
                 part = squares[i][d * 2 * PIECE:(d + 1) * 2 * PIECE]
@@ -160,6 +157,10 @@
             @pl.when(s == nz - 1)
             def _(d=d):
                 sq_in[z, d, p] = sq_out[v, d]
+
+        for d, cc, src, lo in parts:
+            q_s[at(d, cc, src), :] = outs[0][lo:lo + PIECE]
+            k_f[at(d, cc, src), :] = outs[1][lo:lo + PIECE].astype(F32)
 
     def project_rest(v):
         s, p = v // pieces, lax.rem(v, pieces)
@@ -174,14 +175,17 @@
                 for j in range(heads):
                     k_f[at, j * HEAD_DIM:(j + 1) * HEAD_DIM] = done[j]
 
+    def sent_bytes(ref, sem):
+        remote(ref, ref, sem, sem, sib).wait_send()
+
     def drain(u):
-        for d in range(2):
-            pair_copy(u, d).wait_send()
-
-            @pl.when(u < units - pieces)
-            def _(d=d):
-                ring_copy(u, d).wait_send()
-                sq_copy(u, d, 0, sib).wait_send()
+        both = hbuf.at[u, pl.ds(0, 2 * PIECE)]
+        sent_bytes(both, dd_send.at[lax.rem(u, 4)])
+
+        @pl.when(u < units - pieces)
+        def _():
+            sent_bytes(both, ag_send.at[lax.rem(u, 4)])
+            sent_bytes(sq_out.at[u], sq_send.at[lax.rem(u, 4)])
 
     def gather_step(u, _):
         @pl.when(u >= pieces)
@@ -216,13 +220,14 @@
         total = total + sq_in[i]
     sums[me] = total
 
-    def inv_copy(i):
-        dev = lax.rem(me + i, n)
-        return remote(sums.at[me], sums.at[me], iv_send, iv_recv, dev)
-
     def inv_start(i, _):
-        inv_copy(i).start()
+        dev = lax.rem(me + n // 2 + i // 2 * (1 - 2 * lax.rem(i, 2)) + n, n)
+        remote(sums.at[me], sums.at[me], iv_send, iv_recv.at[z], dev).start()
         return 0
+
+    def sums_of(offset):
+        at = sums.at[pl.ds(0, 1 if offset == 0 else 2)]
+        wait_bytes(at, iv_recv.at[chip(offset)])
 
     lax.fori_loop(1, n, inv_start, 0)
     project_rest(units - 1)
@@ -233,10 +238,6 @@
         return 0
 
     lax.fori_loop(0, q_s.shape[0] // k_tile, turn_values, 0)
-    others = sums.at[pl.ds(0, n - 1)]
-    wait_bytes(others, iv_recv)
-    remote(others, others, iv_send, iv_recv, sib).wait_send()
-
     def row_scale(which, src, d, p):
         own = lax.rem(src + (nz - 1 if d == 0 else 1), nz) * 2
         total = sums[own, d, p][which:which + 1] + sums[own + 1, d, p][which:which + 1]
@@ -245,7 +246,7 @@
     def piece_rows(src, cc, d, p):
         return rows((2 * src + cc) * n_rows + d * half + p * PIECE, PIECE)
 
-    def finish_keys(src, _):
+    def finish_keys(src):
         for d in range(2):
             for p in range(pieces):
                 scale = row_scale(1, src, d, p)
@@ -254,9 +255,20 @@
                     for j in range(heads):
                         lanes = slice(j * HEAD_DIM, (j + 1) * HEAD_DIM)
                         k_s[at, lanes] = (k_f[at, lanes] * scale[cc * PIECE:(cc + 1) * PIECE]).astype(BF16)
-        return 0
-
-    lax.fori_loop(0, nz, finish_keys, 0)
+
+    def finish_near(distance):
+        for offset in sorted({distance, -distance % nz}):
+            finish_keys(chip(offset))
+
+    sums_of(0)
+    for distance in range(1, nz // 2 + 1):
+        for offset in sorted({distance, -distance % nz}):
+            sums_of(offset)
+        finish_near(distance - 1)
+        if distance == nz // 2 - 1:
+            finish_near(nz // 2)
+    others = sums.at[pl.ds(0, n - 1)]
+    sent_bytes(others, iv_send)
 
     scale = HEAD_DIM ** -0.5 * math.log2(math.e)
 
@@ -308,36 +320,39 @@
             _, l, acc = carry[j]
             o_s[:, j * HEAD_DIM:(j + 1) * HEAD_DIM] = (acc / l).T.astype(BF16)
 
-    def share_copy(t, d, p):
+    y_tile, e_tile = min(width, 1024), min(width, 2048)
+
+    def share_copy(t, d, p, at):
         return remote(
-            ybuf.at[1, d, pl.ds(p * PIECE, PIECE)], hbuf.at[shares + t, pl.ds(d * half + p * PIECE, PIECE)],
+            ybuf.at[1, d, pl.ds(p * PIECE, PIECE), at], hbuf.at[shares + t, pl.ds(d * half + p * PIECE, PIECE), at],
             sb_send.at[d * pieces + p], sb_recv.at[t, p], sib)
 
-    y_tile, e_tile = min(width, 1024), min(width, 2048)
+    def share_sent(d, p):
+        share_copy(0, d, p, pl.ds(0, width)).wait_send()
 
     def emit(t, d, p):
         @pl.when(t >= 1)
         def _():
-            share_copy(t - 1, d, p).wait_send()
+            share_sent(d, p)
 
         def column(i, _):
             at = rows(i * e_tile, e_tile)
             y = jnp.dot(o_s[...], wo[:, at], preferred_element_type=F32).astype(BF16)
             for cc in range(2):
                 ybuf[cc + c - 2 * cc * c, d, pl.ds(p * PIECE, PIECE), at] = y[cc * PIECE:(cc + 1) * PIECE]
+            share_copy(t, d, p, at).start()
             return 0
 
         lax.fori_loop(0, width // e_tile, column, 0)
-        share_copy(t, d, p).start()
 
     def sum_copy(s, d, k):
         at = rows(d * half + k * sub, sub)
-        return remote(hbuf.at[s, at], hbuf.at[s + 1, at], rs_send.at[d * SUM_PIECES + k],
+        return remote(hbuf.at[s, at], hbuf.at[s + 1, at], rs_send.at[k],
                       rs_recv.at[s, k], toward(d) * 2 + c)
 
     def out_copy(d, k):
         at = rows(d * half + k * sub, sub)
-        return pltpu.make_async_copy(hbuf.at[nz - 1, at], out_hbm.at[at], out_sem.at[d * SUM_PIECES + k])
+        return pltpu.make_async_copy(hbuf.at[nz - 1, at], out_hbm.at[at], out_sem)
 
     def add_up(s, k):
         if k * sub % PIECE == 0:
@@ -366,9 +381,10 @@
 
             lax.fori_loop(0, width // y_tile, column, 0)
 
-            @pl.when(s >= 1)
-            def _(d=d):
-                sum_copy(s - 1, d, k).wait_send()
+            if d == 0:
+                @pl.when(s >= 1)
+                def _():
+                    sent_bytes(hbuf.at[s - 1, pl.ds(0, 2 * sub)], rs_send.at[k])
 
             @pl.when(s < nz - 1)
             def _(d=d):
@@ -423,9 +439,8 @@
 
     for d in range(2):
         for p in range(pieces):
-            share_copy(nz - 1, d, p).wait_send()
-        for k in range(SUM_PIECES):
-            out_copy(d, k).wait()
+            share_sent(d, p)
+    pltpu.make_async_copy(hbuf.at[nz - 1], out_hbm, out_sem).wait()
     for i in (nz * SUM_PIECES - 2, nz * SUM_PIECES - 1):
         for which in range(2):
             cache_copy(i, which).wait()
@@ -478,10 +493,10 @@
                 pltpu.VMEM((nz, 2, pieces, 2, 2 * PIECE), F32),
                 pltpu.VMEM((n, 2, pieces, 2, 2 * PIECE), F32),
                 dma((4 + 2 * pieces,)),
-                dma((4, 2)), dma((units,)), dma((4, 2)), dma((units,)),
-                dma((4, 2)), dma, dma, dma,
-                dma((2 * SUM_PIECES,)), dma((nz - 1, SUM_PIECES)),
-                dma((2 * pieces,)), dma((nz, pieces)), dma((2, 2)), dma((2 * SUM_PIECES,)),
+                dma((4,)), dma((units - pieces,)), dma((4,)), dma((units,)),
+                dma((4,)), dma, dma, dma((nz,)),
+                dma((SUM_PIECES,)), dma((nz - 1, SUM_PIECES)),
+                dma((2 * pieces,)), dma((nz, pieces)), dma((2, 2)), dma,
             ],
             compiler_params=pltpu.CompilerParams(
                 collective_id=0, has_side_effects=True, vmem_limit_bytes=KERNEL_VMEM),

time: 351 us -> 349 us (level)
  no operation moved by 1% of the time
where the time goes in v5:
time: 349 us
  Pallas kernels  348 us (100%)
    pallas_call x1, Pallas kernels, local_block(): pl.pallas_call(functools.partial(block_kernel, n), out_shape=tuple((pltpu...  346 us

profile of v5, /device:TPU:21, one launch (start us, length us, event | category | flops | bytes accessed | tf_op | source)
XLA Modules:
  0.0 348.9 jit_solution(15815004530624587152)
XLA Ops:
  0.6 345.6 %attention_block.1 = (bf16[256,4096]{1,0:T(8,128)(2,1)S(1)}, bf16[4096,2,128]{2,1,0:T(2,128)(2,1)S(1)}, bf16[4096,2,128]{2,1,0:T(2,128)(2,1)S(1)}) custom-call(bf16[256,4096]{1,0:T(8,128)(2,1)} %bitcast.7, f32[1,4096]{1,0:T(1,128)} %bitcast.8, bf16[4096,256]{1,0:T(8,128)(2,1)} %wq_hbm.1, bf16[4096,256]{1,0:T(8,128)(2,1)} %wk_hbm.1, ...), custom_call_target="tpu_custom_call" | custom-call | tf_op jit(solution)/shard_map/attention_block/pallas_call | solution.py:476
  346.2 2.8 write_out.1

commit v6 on v5

--- a/solution.py
+++ b/solution.py
@@ -26,13 +26,13 @@
     sign = np.concatenate([-np.ones(half), np.ones(half)])
     base = (np.arange(seq_len // PIECE) * PIECE)[:, None] * inv_freq
     off = np.arange(PIECE)[:, None] * inv_freq
-    return [jnp.asarray(t, F32) for t in (np.cos(base), sign * np.sin(base), np.cos(off), sign * np.sin(off))]
+    return jnp.asarray(np.concatenate([np.cos(base), sign * np.sin(base), np.cos(off), sign * np.sin(off)]), F32)
 
 
 def block_kernel(
-    n, x_hbm, gain, wq_hbm, wk_hbm, wv_hbm, wo_hbm, q_gain, k_gain, cos_b, sin_b, cos_o, sin_o,
+    n, x_hbm, gain_hbm, wq_hbm, wk_hbm, wv_hbm, wo_hbm, q_gain_hbm, k_gain_hbm, turns_hbm,
     out_hbm, k_hbm, v_hbm,
-    hbuf, wqkv, wo, q_s, k_f, v_s, v_t, ybuf, o_s, kv_st, sq_out, sq_in, sums,
+    gain, q_gain, k_gain, turns, hbuf, wqkv, wo, q_s, k_f, v_s, v_t, ybuf, o_s, kv_st, sq_out, sq_in, sums,
     ld_sem, ag_send, ag_recv, dd_send, dd_recv, sq_send, sq_recv, iv_send, iv_recv,
     rs_send, rs_recv, sb_send, sb_recv, st_sem, out_sem,
 ):
@@ -53,6 +53,11 @@
 
     k_s = wqkv.at[0]
 
+    n_base = q_s.shape[0] // PIECE
+    starts = (0, n_base, 2 * n_base, 2 * n_base + PIECE)
+    cos_b, sin_b, cos_o, sin_o = (
+        turns.at[pl.ds(start, size)] for start, size in zip(starts, (n_base, n_base, PIECE, PIECE)))
+
     def chip(offset):
         return lax.rem(z + offset + 2 * nz, nz)
 
@@ -74,11 +79,15 @@
         at = pl.ds(d * half + p * PIECE, PIECE)
         return pltpu.make_async_copy(x_hbm.at[at], ybuf.at[0, d, pl.ds(p * PIECE, PIECE)], ld_sem.at[4 + d * pieces + p])
 
+    gain_load = pltpu.make_async_copy(gain_hbm, gain, ld_sem.at[4 + 2 * pieces])
+    gain_load.start()
     for p in range(pieces):
         for d in range(2):
             x_load(d, p).start()
     loads = [pltpu.make_async_copy(w, wqkv.at[i, pl.ds(0, width)], ld_sem.at[i]) for i, w in enumerate((wq_hbm, wk_hbm, wv_hbm))]
     loads.append(pltpu.make_async_copy(wo_hbm, wo, ld_sem.at[3]))
+    for i, (src, dst) in enumerate(((q_gain_hbm, q_gain), (k_gain_hbm, k_gain), (turns_hbm, turns))):
+        loads.append(pltpu.make_async_copy(src, dst, ld_sem.at[5 + 2 * pieces + i]))
 
     barrier = pltpu.get_barrier_semaphore()
 
@@ -94,6 +103,7 @@
     def pair_copy(u, d):
         return remote(quarter(u, d), quarter(u, d), dd_send.at[lax.rem(u, 4)], dd_recv.at[u], sib)
 
+    gain_load.wait()
     for p in range(pieces):
         for d in range(2):
             x_load(d, p).wait()
@@ -468,17 +478,20 @@
         seq_len = n * n_rows
         nz, pieces = n // 2, n_rows // 2 // PIECE
         units = nz * pieces
-        tables = rope_constants(seq_len)
+        turns = rope_constants(seq_len)
         shapes = ((n_rows, width),) + ((seq_len, cols // HEAD_DIM, HEAD_DIM),) * 2
         any_spec = pl.BlockSpec(memory_space=pl.ANY)
-        vmem_spec = pl.BlockSpec(memory_space=pltpu.VMEM)
         dma = pltpu.SemaphoreType.DMA
         held = pl.pallas_call(
             functools.partial(block_kernel, n),
             out_shape=tuple(pltpu.VMEM(shape, BF16) for shape in shapes),
-            in_specs=[any_spec, vmem_spec] + [any_spec] * 4 + [vmem_spec] * 6,
+            in_specs=[any_spec] * 9,
             out_specs=(any_spec,) * 3,
             scratch_shapes=[
+                pltpu.VMEM((1, width), F32),
+                pltpu.VMEM((1, cols), F32),
+                pltpu.VMEM((1, cols), F32),
+                pltpu.VMEM(turns.shape, F32),
                 pltpu.VMEM((units, 4 * PIECE, width), BF16),
                 pltpu.VMEM((3, max(width, seq_len), cols), BF16),
                 pltpu.VMEM((cols, width), BF16),
@@ -492,7 +505,7 @@
                 pltpu.VMEM((units, 2, 2, 2 * PIECE), F32),
                 pltpu.VMEM((nz, 2, pieces, 2, 2 * PIECE), F32),
                 pltpu.VMEM((n, 2, pieces, 2, 2 * PIECE), F32),
-                dma((4 + 2 * pieces,)),
+                dma((8 + 2 * pieces,)),
                 dma((4,)), dma((units - pieces,)), dma((4,)), dma((units,)),
                 dma((4,)), dma, dma, dma((nz,)),
                 dma((SUM_PIECES,)), dma((nz - 1, SUM_PIECES)),
@@ -501,7 +514,7 @@
             compiler_params=pltpu.CompilerParams(
                 collective_id=0, has_side_effects=True, vmem_limit_bytes=KERNEL_VMEM),
             name="attention_block",
-        )(x_local[0], attn_gain[None], wq, wk, wv, wo, q_gain[None], k_gain[None], *tables)
+        )(x_local[0], attn_gain[None], wq, wk, wv, wo, q_gain[None], k_gain[None], turns)
         out, k_rot, v_rows = pl.pallas_call(
             flush_kernel,
             out_shape=tuple(jax.ShapeDtypeStruct(shape, BF16) for shape in shapes),

time: 349 us -> 348 us (level)
  no operation moved by 1% of the time
where the time goes in v6:
time: 348 us
  Pallas kernels  348 us (100%)
    pallas_call x1, Pallas kernels, local_block(): pl.pallas_call(functools.partial(block_kernel, n), out_shape=tuple((pltpu...  345 us

profile of v6, /device:TPU:21, one launch (start us, length us, event | category | flops | bytes accessed | tf_op | source)
XLA Modules:
  0.0 348.2 jit_solution(688300106697219289)
XLA Ops:
  0.6 344.8 %attention_block.1 = (bf16[256,4096]{1,0:T(8,128)(2,1)S(1)}, bf16[4096,2,128]{2,1,0:T(2,128)(2,1)S(1)}, bf16[4096,2,128]{2,1,0:T(2,128)(2,1)S(1)}) custom-call(bf16[256,4096]{1,0:T(8,128)(2,1)} %bitcast.7, f32[1,4096]{1,0:T(1,128)} %bitcast.8, bf16[4096,256]{1,0:T(8,128)(2,1)} %wq_hbm.1, bf16[4096,256]{1,0:T(8,128)(2,1)} %wk_hbm.1, ...), custom_call_target="tpu_custom_call" | custom-call | tf_op jit(solution)/shard_map/attention_block/pallas_call | solution.py:485
  345.4 2.8 write_out.1
